TPU v7x, 128 devices: a whole 4x4x4 slice. The times are simulated.
128 devices in a mesh: rep: 1, r: 4 (over x), s: 32 (over y, z, core).
Axes of the slice: x: 4, y: 4, z: 4, core: 2. Of those that a mesh axis runs over, the one named last changes fastest.
Arguments:
- x: bfloat16 [128, 2048, 1280], P(('rep', 'r', 's'))
- dy: bfloat16 [128, 2048, 1280], P(('rep', 'r', 's'))
- w_gate: bfloat16 [2, 1280, 4480], P(None, 's')
- w_up: bfloat16 [2, 1280, 4480], P(None, 's')
- w_down: bfloat16 [2, 4480, 1280], P(None, 's')
- m_w_gate: float32 [2, 1280, 4480], P(None, 's')
- m_w_up: float32 [2, 1280, 4480], P(None, 's')
- m_w_down: float32 [2, 4480, 1280], P(None, 's')
- v_w_gate: float32 [2, 1280, 4480], P(None, 's')
- v_w_up: float32 [2, 1280, 4480], P(None, 's')
- v_w_down: float32 [2, 4480, 1280], P(None, 's')
Outputs:
- output 1: bfloat16 [2, 1280, 4480], P('rep', 's')
- output 2: bfloat16 [2, 1280, 4480], P('rep', 's')
- output 3: bfloat16 [2, 4480, 1280], P('rep', 's')
- output 4: float32 [2, 1280, 4480], P('rep', 's')
- output 5: float32 [2, 1280, 4480], P('rep', 's')
- output 6: float32 [2, 4480, 1280], P('rep', 's')
- output 7: float32 [2, 1280, 4480], P('rep', 's')
- output 8: float32 [2, 1280, 4480], P('rep', 's')
- output 9: float32 [2, 4480, 1280], P('rep', 's')
All inputs are finite; a program needn't handle non-finite values.
Results may differ from a plain program's by a relative error of at most 0.022.
Values are sent between devices in bfloat16 or wider.
A program may use at most 1.5 GiB of HBM per device.

v0:
```python
import jax
import jax.numpy as jnp
from jax import lax
from jax.sharding import PartitionSpec as P

NAMES = ("w_gate", "w_up", "w_down")


def matmul(a, w):
    return jnp.dot(a, w, preferred_element_type=jnp.float32).astype(jnp.bfloat16)


def normed(h):
    wide = h.astype(jnp.float32)
    scale = lax.rsqrt(jnp.mean(wide**2, -1, keepdims=True) + 1e-6)
    return (wide * scale).astype(jnp.bfloat16)


def layer(h, w):
    a = normed(h)
    gate = jnp.dot(a, w["w_gate"], preferred_element_type=jnp.float32)
    up = jnp.dot(a, w["w_up"], preferred_element_type=jnp.float32)
    return h + matmul((jax.nn.silu(gate) * up).astype(jnp.bfloat16), w["w_down"])


def adamw(w, m, v, g):
    m = 0.9 * m + 0.1 * g
    v = 0.95 * v + 0.05 * g * g
    step = m * lax.rsqrt(v + 1e-8) + 0.1 * w
    return (w - 0.02 * step).astype(jnp.bfloat16), m, v


def clipped(gradients, sum_of_squares, count):
    factor = jnp.minimum(1.0, 0.5 * lax.rsqrt(sum_of_squares / count + 1e-30))
    return [g * factor for g in gradients]


def solution(mesh):
    def fetched(weights, number):
        return {name: lax.all_gather(w[number], "s", axis=0, tiled=True) for name, w in zip(NAMES, weights, strict=True)}

    def summed(term):
        return lax.psum(lax.psum_scatter(term, "s", scatter_dimension=0, tiled=True), "r")

    def step(x, dy, *arrays):
        weights, m, v = (arrays[i : i + 3] for i in (0, 3, 6))
        layers = weights[0].shape[0]
        h, kept = x[0], []
        for number in range(layers):
            kept.append(h)
            h = layer(h, fetched(weights, number))
        by_h, mine = dy[0], [None] * layers
        for number in reversed(range(layers)):
            _, back = jax.vjp(lambda w, h: layer(h, w), fetched(weights, number), kept[number])
            by_w, by_h = back(by_h)
            mine[number] = [summed(by_w[name]) for name in NAMES]
        gradients = [jnp.stack([mine[number][i] for number in range(layers)]).astype(jnp.float32) for i in range(3)]
        squares = lax.psum(sum(jnp.sum(g * g) for g in gradients), "s")
        gradients = clipped(gradients, squares, lax.psum(1, "s") * sum(g.size for g in gradients))
        new = [adamw(w.astype(jnp.float32), m, v, g) for w, m, v, g in zip(weights, m, v, gradients, strict=True)]
        return tuple(one[which] for which in range(3) for one in new)

    states, cut = P(("rep", "r", "s"), None, None), P(None, "s", None)
    return jax.shard_map(
        step,
        mesh=mesh,
        in_specs=(states, states) + (cut,) * 9,
        out_specs=(P("rep", "s", None),) * 9,
        check_vma=False,
    )
```

profile of v0, /device:TPU:1, one launch (start us, length us, event | category | flops | bytes accessed | tf_op | source)
XLA Modules:
  0.0 1396.6 jit_solution(7539990690133620166)
XLA Ops:
  11.4 3.7 fusion.107
  16.9 8.0 copy.38
  28.4 7.9 copy.39
  36.3 37.9 %all-gather.13.cloned.1.call-done = bf16[1,1280,4480]{2,1,0:T(8,128)(2,1)} async-done(((bf16[1,40,4480]{2,1,0:T(8,128)(2,1)}), bf16[1,1280,4480]{2,1,0:T(8,128)(2,1)}) %all-gather.13.cloned.1.call-update) | async-done | bytes 11468816 | tf_op jit(solution)/shard_map/all_gather | solution.py:40
  74.3 32.0 %fusion.35 = f32[2048,4480]{1,0:T(8,128)} fusion(bf16[1,1280,4480]{2,1,0:T(8,128)(2,1)} %all-gather.13.cloned.1.call-done, bf16[1,2048,1280]{1,2,0:T(8,128)(2,1)} %copy.38, f32[2048]{0:T(1024)S(1)} %add_rsqrt_fusion), kind=kOutput, calls=%fused_computation.52 | convolution fusion | flops 23495966720 | bytes 53420032 | tf_op jit(solution)/shard_map/dot_general | solution.py:21
  106.3 30.2 %all-gather.15.cloned.1.call-done = bf16[1,1280,4480]{2,1,0:T(8,128)(2,1)} async-done(((bf16[1,40,4480]{2,1,0:T(8,128)(2,1)}), bf16[1,1280,4480]{2,1,0:T(8,128)(2,1)}) %all-gather.15.cloned.1.call-update) | async-done | bytes 11468816 | tf_op jit(solution)/shard_map/all_gather | solution.py:40
  136.4 45.2 %multiply_convert_fusion.1 = (bf16[2048,4480]{1,0:T(8,128)(2,1)}, f32[2048,4480]{1,0:T(8,128)}) fusion(f32[2048,4480]{1,0:T(8,128)} %fusion.35, bf16[1,1280,4480]{2,1,0:T(8,128)(2,1)} %all-gather.15.cloned.1.call-done, bf16[1,2048,1280]{1,2,0:T(8,128)(2,1)} %copy.38, f32[2048]{0:T(1024)S(1)} %add_rsqrt_fusion), kind=kOutput, calls=%fused_computation.17 | convolution fusion | flops 23551016960 | bytes 108470272 | tf_op jit(solution)/shard_map/dot_general | solution.py:22
  181.6 43.8 %all-gather.17.cloned.1.call-done = bf16[1,4480,1280]{2,0,1:T(2,128)(2,1)} async-done(((bf16[1,140,1280]{2,0,1:T(2,128)(2,1)}), bf16[1,4480,1280]{2,0,1:T(2,128)(2,1)}) %all-gather.17.cloned.1.call-update) | async-done | bytes 11468816 | tf_op jit(solution)/shard_map/all_gather | solution.py:40
  225.5 46.5 %fusion.41 = (f32[2048]{0:T(1024)S(1)}, bf16[2048,1280]{0,1:T(8,128)(2,1)}) fusion(bf16[2048,4480]{1,0:T(8,128)(2,1)} %get-tuple-element.61, bf16[1,4480,1280]{2,0,1:T(2,128)(2,1)} %all-gather.17.cloned.1.call-done, bf16[1,2048,1280]{1,2,0:T(8,128)(2,1)} %copy.38), kind=kOutput, calls=%fused_computation.58 | convolution fusion | flops 23501207552 | bytes 40312832 | tf_op jit(solution)/shard_map/dot_general | solution.py:10
  271.9 42.3 %all-gather.21.cloned.1.call-done = bf16[1,4480,1280]{2,0,1:T(2,128)(2,1)} async-done(((bf16[1,140,1280]{2,0,1:T(2,128)(2,1)}), bf16[1,4480,1280]{2,0,1:T(2,128)(2,1)}) %all-gather.21.cloned.1.call-update) | async-done | bytes 11468816 | tf_op jit(solution)/shard_map/all_gather | solution.py:40
  314.2 33.1 %convolution_convert_fusion.1 = bf16[2048,4480]{1,0:T(8,128)(2,1)} fusion(bf16[1,4480,1280]{2,0,1:T(2,128)(2,1)} %all-gather.21.cloned.1.call-done, bf16[1,2048,1280]{2,1,0:T(8,128)(2,1)} %param.12), kind=kOutput, calls=%fused_computation.26 | convolution fusion | flops 23497277440 | bytes 35061760 | tf_op jit(solution)/shard_map/transpose(jvp())/dot_general | solution.py:10
  347.3 28.7 %all-gather.23.cloned.1.call-done = bf16[1,1280,4480]{2,1,0:T(8,128)(2,1)} async-done(((bf16[1,40,4480]{2,1,0:T(8,128)(2,1)}), bf16[1,1280,4480]{2,1,0:T(8,128)(2,1)}) %all-gather.23.cloned.1.call-update) | async-done | bytes 11468816 | tf_op jit(solution)/shard_map/all_gather | solution.py:40
  376.1 32.1 %fusion.26 = f32[2048,4480]{1,0:T(8,128)} fusion(bf16[1,1280,4480]{2,1,0:T(8,128)(2,1)} %all-gather.23.cloned.1.call-done, bf16[2048,1280]{0,1:T(8,128)(2,1)} %get-tuple-element.64, f32[2048]{0:T(1024)S(1)} %fusion.94), kind=kOutput, calls=%fused_computation.43 | convolution fusion | flops 23495966720 | bytes 53420032 | tf_op jit(solution)/shard_map/jvp()/dot_general | solution.py:22
  408.1 30.0 %all-gather.19.cloned.1.call-done = bf16[1,1280,4480]{2,1,0:T(8,128)(2,1)} async-done(((bf16[1,40,4480]{2,1,0:T(8,128)(2,1)}), bf16[1,1280,4480]{2,1,0:T(8,128)(2,1)}) %all-gather.19.cloned.1.call-update) | async-done | bytes 11468816 | tf_op jit(solution)/shard_map/all_gather | solution.py:40
  438.1 53.9 %fusion.4 = (bf16[2048,4480]{1,0:T(8,128)(2,1)}, f32[2048,4480]{1,0:T(8,128)}) fusion(f32[2048,4480]{1,0:T(8,128)} %fusion.26, bf16[2048,4480]{1,0:T(8,128)(2,1)} %convolution_convert_fusion.1, bf16[1,1280,4480]{2,1,0:T(8,128)(2,1)} %all-gather.19.cloned.1.call-done, bf16[2048,1280]{0,1:T(8,128)(2,1)} %get-tuple-element.64, f32[2048]{0:T(1024)S(1)} %fusion.94), kind=kOutput, calls=%fused_computation.8 | convolution fusion | flops 23606067200 | bytes 126820352 | tf_op jit(solution)/shard_map/jvp()/dot_general | solution.py:21
  492.0 35.5 %fusion.47 = bf16[2048,1280]{0,1:T(8,128)(2,1)} fusion(bf16[1,1280,4480]{2,1,0:T(8,128)(2,1)} %all-gather.23.cloned.1.call-done, bf16[2048,4480]{1,0:T(8,128)(2,1)} %convolution_convert_fusion.1, f32[2048,4480]{1,0:T(8,128)} %get-tuple-element.66), kind=kOutput, calls=%fused_computation.62 | convolution fusion | flops 23545774080 | bytes 71761920 | tf_op jit(solution)/shard_map/transpose(jvp())/dot_general | solution.py:22
  527.4 34.2 %fusion.43 = (f32[2048]{0:T(1024)S(1)}, bf16[2048,1280]{0,1:T(8,128)(2,1)}) fusion(bf16[2048,1280]{0,1:T(8,128)(2,1)} %get-tuple-element.64, bf16[2048,1280]{0,1:T(8,128)(2,1)} %fusion.47, bf16[2048,4480]{1,0:T(8,128)(2,1)} %get-tuple-element.65, bf16[1,1280,4480]{2,1,0:T(8,128)(2,1)} %all-gather.19.cloned.1.call-done), kind=kOutput, calls=%fused_computation.60 | convolution fusion | flops 23501207552 | bytes 45555712 | tf_op jit(solution)/shard_map/transpose(jvp())/dot_general | solution.py:21
  561.7 12.3 fusion.60
  574.0 32.8 %convolution_convert_fusion = bf16[2048,4480]{1,0:T(8,128)(2,1)} fusion(bf16[2048,1280]{0,1:T(8,128)(2,1)} %fusion.60, bf16[1,4480,1280]{2,0,1:T(2,128)(2,1)} %all-gather.17.cloned.1.call-done), kind=kOutput, calls=%fused_computation.25 | convolution fusion | flops 23497277440 | bytes 35061760 | tf_op jit(solution)/shard_map/transpose(jvp())/dot_general | solution.py:10
  606.8 37.5 %fusion.19 = bf16[1280,4480]{1,0:T(8,128)(2,1)} fusion(bf16[2048,4480]{1,0:T(8,128)(2,1)} %convolution_convert_fusion, f32[2048,4480]{1,0:T(8,128)} %fusion.35, bf16[1,2048,1280]{1,2,0:T(8,128)(2,1)} %copy.38, f32[2048]{0:T(1024)S(1)} %copy-done.14), kind=kOutput, calls=%fused_computation.24 | convolution fusion | flops 23556751360 | bytes 71770112 | tf_op jit(solution)/shard_map/transpose(jvp())/dot_general | solution.py:22
  644.4 37.8 %fusion.15 = bf16[1280,4480]{1,0:T(8,128)(2,1)} fusion(bf16[2048,4480]{1,0:T(8,128)(2,1)} %convolution_convert_fusion.1, bf16[2048,1280]{0,1:T(8,128)(2,1)} %get-tuple-element.64, f32[2048]{0:T(1024)S(1)} %fusion.94, f32[2048,4480]{1,0:T(8,128)} %get-tuple-element.66), kind=kOutput, calls=%fused_computation.22 | convolution fusion | flops 23556751360 | bytes 71770112 | tf_op jit(solution)/shard_map/transpose(jvp())/dot_general | solution.py:22
  682.3 44.5 %fusion.16 = bf16[1280,4480]{1,0:T(8,128)(2,1)} fusion(f32[2048,4480]{1,0:T(8,128)} %fusion.35, f32[2048,4480]{1,0:T(8,128)} %get-tuple-element.62, bf16[2048,4480]{1,0:T(8,128)(2,1)} %convolution_convert_fusion, bf16[1,2048,1280]{1,2,0:T(8,128)(2,1)} %copy.38, f32[2048]{0:T(1024)S(1)} %copy-done.14), kind=kOutput, calls=%fused_computation.23 | convolution fusion | flops 23602626560 | bytes 108470272 | tf_op jit(solution)/shard_map/transpose(jvp())/dot_general | solution.py:21
  726.8 31.2 %convolution_convert_fusion.4 = bf16[1280,4480]{1,0:T(8,128)(2,1)} fusion(bf16[2048,4480]{1,0:T(8,128)(2,1)} %get-tuple-element.65, bf16[2048,1280]{0,1:T(8,128)(2,1)} %get-tuple-element.64, f32[2048]{0:T(1024)S(1)} %fusion.94), kind=kOutput, calls=%fused_computation.29 | convolution fusion | flops 23495966720 | bytes 35069952 | tf_op jit(solution)/shard_map/transpose(jvp())/dot_general | solution.py:21
  758.1 30.1 %convolution_convert_fusion.3 = bf16[4480,1280]{1,0:T(8,128)(2,1)} fusion(bf16[2048,4480]{1,0:T(8,128)(2,1)} %get-tuple-element.61, bf16[2048,1280]{0,1:T(8,128)(2,1)} %fusion.60), kind=kOutput, calls=%fused_computation.28 | convolution fusion | flops 23493836800 | bytes 35061760 | tf_op jit(solution)/shard_map/transpose(jvp())/dot_general | solution.py:10
  788.2 38.6 %convolution_convert_fusion.2 = bf16[4480,1280]{1,0:T(8,128)(2,1)} fusion(f32[2048,4480]{1,0:T(8,128)} %fusion.26, bf16[1,2048,1280]{2,1,0:T(8,128)(2,1)} %param.12, f32[2048,4480]{1,0:T(8,128)} %get-tuple-element.66), kind=kOutput, calls=%fused_computation.27 | convolution fusion | flops 23548887040 | bytes 90112000 | tf_op jit(solution)/shard_map/transpose(jvp())/dot_general | solution.py:10
  826.8 146.2 %fusion.100 = (bf16[144,1280]{1,0:T(8,128)(2,1)S(1)}, bf16[144,1280]{1,0:T(8,128)(2,1)S(1)}) fusion(bf16[4480,1280]{1,0:T(8,128)(2,1)} %convolution_convert_fusion.2, bf16[4480,1280]{1,0:T(8,128)(2,1)} %convolution_convert_fusion.3), kind=kCustom, calls=%all-reduce-scatter.2 | all-reduce-scatter fusion | flops 11796481 | bytes 23675392
  973.1 4.5 collective-permute-start
  989.7 11.9 reduce-scatter.23.cloned.1.call-done
  1001.7 119.4 %reduce-scatter.17.cloned.1.call-done = bf16[40,4480]{1,0:T(8,128)(2,1)} async-done(((bf16[1280,4480]{1,0:T(8,128)(2,1)}), bf16[40,4480]{1,0:T(8,128)(2,1)}) %reduce-scatter.17.cloned.1.call-update) | async-done | bytes 358416
  1121.1 119.3 %reduce-scatter.19.cloned.1.call-done = bf16[40,4480]{1,0:T(8,128)(2,1)} async-done(((bf16[1280,4480]{1,0:T(8,128)(2,1)}), bf16[40,4480]{1,0:T(8,128)(2,1)}) %reduce-scatter.19.cloned.1.call-update) | async-done | bytes 358416
  1240.4 64.0 %all-reduce.12.cloned.1.call-done = (bf16[1,40,4480]{2,1,0:T(8,128)(2,1)}, bf16[1,40,4480]{2,1,0:T(8,128)(2,1)}, bf16[1,40,4480]{2,1,0:T(8,128)(2,1)}, bf16[1,40...) async-done(((bf16[1,40,4480]{2,1,0:T(8,128)(2,1)}, bf16[1,40,4480]{2,1,0:T(8,128)(2,1)}, bf16[1,40,4480]{2,1,0:T(8,128)(2,1)}, ...) | async-done | bytes 2150416 | tf_op jit(solution)/shard_map/psum | solution.py:43
  1312.6 63.9 %psum.55 = f32[]{:T(128)} all-reduce(f32[]{:T(128)S(6)} %add.111), channel_id=1, replica_groups=mesh['rep'=1,'r'=4,'s'=32] {'s'}, use_global_device_ids=true, to_apply=%region_18.19 | all-reduce | flops 1 | bytes 8 | tf_op jit(solution)/shard_map/psum | solution.py:58
  (79 shorter events, 39.9 us)
Async XLA Ops:
  7.2 67.1 %all-gather.13.cloned.1.call-start = ((), (), s32[]{:S(2)}) async-start(), calls=%async_computation.4 | async-start | bytes 11827200 | tf_op jit(solution)/shard_map/all_gather | solution.py:40
  9.2 127.2 %all-gather.15.cloned.1.call-start = ((), (), s32[]{:S(2)}) async-start(), calls=%async_computation.5 | async-start | bytes 11827200 | tf_op jit(solution)/shard_map/all_gather | solution.py:40
  11.3 214.1 %all-gather.17.cloned.1.call-start = ((), (), s32[]{:S(2)}) async-start(), calls=%async_computation.6 | async-start | bytes 23654400 | tf_op jit(solution)/shard_map/all_gather | solution.py:40
  15.1 299.1 %all-gather.21.cloned.1.call-start = ((), (), s32[]{:S(2)}) async-start(), calls=%async_computation.8 | async-start | bytes 23654400 | tf_op jit(solution)/shard_map/all_gather | solution.py:40
  15.6 360.4 %all-gather.23.cloned.1.call-start = ((), (), s32[]{:S(2)}) async-start(), calls=%async_computation.9 | async-start | bytes 11827200 | tf_op jit(solution)/shard_map/all_gather | solution.py:40
  16.2 421.8 %all-gather.19.cloned.1.call-start = ((), (), s32[]{:S(2)}) async-start(), calls=%async_computation.7 | async-start | bytes 11827200 | tf_op jit(solution)/shard_map/all_gather | solution.py:40
  16.8 972.9 %reduce-scatter.21.cloned.1.call-start = ((), (), s32[]{:S(2)}) async-start(), calls=%async_computation.12 | async-start | bytes 11827200
  28.4 108.0 %copy-start.13 = (f32[2048]{0:T(1024)}, f32[2048]{0:T(1024)S(1)}, u32[]{:S(2)}) copy-start(f32[2048]{0:T(1024)S(1)} %add_rsqrt_fusion) | copy-start | bytes 24580
  271.9 75.4 %copy-start.11 = (f32[2048]{0:T(1024)}, f32[2048]{0:T(1024)S(1)}, u32[]{:S(2)}) copy-start(f32[2048]{0:T(1024)S(1)} %get-tuple-element.63) | copy-start | bytes 24580
  527.4 34.2 %copy-start.12 = (f32[2048]{0:T(1024)S(1)}, f32[2048]{0:T(1024)}, u32[]{:S(2)}) copy-start(f32[2048]{0:T(1024)} %copy-done.11) | copy-start | bytes 24580
  574.0 32.8 %copy-start.14 = (f32[2048]{0:T(1024)S(1)}, f32[2048]{0:T(1024)}, u32[]{:S(2)}) copy-start(f32[2048]{0:T(1024)} %copy-done.13) | copy-start | bytes 24580
  644.3 357.4 %reduce-scatter.23.cloned.1.call-start = ((), (), s32[]{:S(2)}) async-start(), calls=%async_computation.13 | async-start | bytes 11827200
  682.2 438.8 %reduce-scatter.17.cloned.1.call-start = ((), (), s32[]{:S(2)}) async-start(), calls=%async_computation.10 | async-start | bytes 11827200
  726.8 513.6 %reduce-scatter.19.cloned.1.call-start = ((), (), s32[]{:S(2)}) async-start(), calls=%async_computation.11 | async-start | bytes 11827200
  758.0 546.3 %all-reduce.12.cloned.1.call-start = ((), (), s32[]{:S(2)}) async-start(), calls=%async_computation.14 | async-start | bytes 4341760 | tf_op jit(solution)/shard_map/psum | solution.py:43
  826.8 152.9 %copy-start.15 = (u32[128]{0:T(128)S(1)}, u32[128]{0:T(128)}, u32[]{:S(2)}) copy-start(u32[128]{0:T(128)} %constant.59) | copy-start | bytes 1540
  973.0 404.1 %copy-start = (bf16[2,140,1280]{2,0,1:T(2,128)(2,1)S(1)}, bf16[2,140,1280]{2,0,1:T(2,128)(2,1)}, u32[]{:S(2)}) copy-start(bf16[2,140,1280]{2,0,1:T(2,128)(2,1)} %param.15) | copy-start | bytes 2150404
  973.1 8.5 collective-permute-start
  977.8 7.4 collective-permute-start.1
  988.0 398.0 %copy-start.1 = (bf16[2,40,4480]{2,1,0:T(8,128)(2,1)S(1)}, bf16[2,40,4480]{2,1,0:T(8,128)(2,1)}, u32[]{:S(2)}) copy-start(bf16[2,40,4480]{2,1,0:T(8,128)(2,1)} %param.13) | copy-start | bytes 2150404
  988.1 398.0 %copy-start.2 = (bf16[2,40,4480]{2,1,0:T(8,128)(2,1)S(1)}, bf16[2,40,4480]{2,1,0:T(8,128)(2,1)}, u32[]{:S(2)}) copy-start(bf16[2,40,4480]{2,1,0:T(8,128)(2,1)} %param.14) | copy-start | bytes 2150404
  1304.3 81.7 %copy-start.7 = (bf16[1,40,4480]{2,1,0:T(8,128)(2,1)S(1)}, bf16[1,40,4480]{2,1,0:T(8,128)(2,1)}, u32[]{:S(2)}) copy-start(bf16[1,40,4480]{2,1,0:T(8,128)(2,1)} %get-tuple-element.36) | copy-start | bytes 1075204
  1304.3 81.7 %copy-start.8 = (bf16[1,40,4480]{2,1,0:T(8,128)(2,1)S(1)}, bf16[1,40,4480]{2,1,0:T(8,128)(2,1)}, u32[]{:S(2)}) copy-start(bf16[1,40,4480]{2,1,0:T(8,128)(2,1)} %get-tuple-element.37) | copy-start | bytes 1075204
  1304.3 81.7 %copy-start.9 = (bf16[1,40,4480]{2,1,0:T(8,128)(2,1)S(1)}, bf16[1,40,4480]{2,1,0:T(8,128)(2,1)}, u32[]{:S(2)}) copy-start(bf16[1,40,4480]{2,1,0:T(8,128)(2,1)} %get-tuple-element.38) | copy-start | bytes 1075204
  1377.2 8.9 copy-start.3
  1377.2 8.9 copy-start.4
  1377.2 8.9 copy-start.5
  1377.2 8.9 copy-start.6
  1377.2 8.9 copy-start.10
Sparse Core Ops, SparseCore 0:
  10.8 63.4 all-gather.12
  77.1 59.2 all-gather.14
  139.3 86.0 all-gather.16
  228.2 85.9 all-gather.20
  316.9 59.1 all-gather.22
  378.7 59.2 all-gather.18
  644.4 113.8 reduce-scatter.20
  762.1 239.4 reduce-scatter.22
  1005.5 115.4 reduce-scatter.16
  1124.7 115.5 reduce-scatter.18
  1243.7 60.5 all-reduce.11
where the time goes:
time: 1410 us; the launch traced here: 1400 us
  matrix products  565 us (40%)
  waiting for transfers between devices  532 us (38%)
  blocking collectives  210 us (15%)
  local copies, waits for them, and re-layouts  36 us (3%)
  other arithmetic  28.8 us (2%)
  between operations  17.9 us (1%)
    unnamed x17, waiting for transfers between devices  255 us
    all_gather x6, waiting for transfers between devices, fetched(): lax.all_gather(w[number], 's', axis=0, tiled=True)  213 us
    dot_general x5, matrix products, layer(): gate = jnp.dot(a, w['w_gate'], preferred_element_type=jnp.float32)  196 us
    dot_general x5, matrix products, layer(): up = jnp.dot(a, w['w_up'], preferred_element_type=jnp.float32)  188 us
    dot_general x5, matrix products, matmul(): jnp.dot(a, w, preferred_element_type=jnp.float32).astype(jnp.bfloat16)  181 us
    unnamed x1, blocking collectives  146 us
    psum x1, waiting for transfers between devices, summed(): lax.psum(lax.psum_scatter(term, 's', scatter_dimension=0, tiled=True), 'r')  64 us
    psum x1, blocking collectives, step(): squares = lax.psum(sum((jnp.sum(g * g) for g in gradients)), 's')  63.9 us
  transfers between devices with their start and end apart: 13, of which 12 were waited for; matrix products, arithmetic and copies ran while one was open for 39% of the time, Pallas kernels for 0%

commit v1 on v0

v1 whole, which is shorter than its diff:
```python
import functools
import types

import jax
import jax.numpy as jnp
from jax import lax
from jax.experimental import pallas as pl
from jax.experimental.pallas import tpu as pltpu
from jax.sharding import Mesh
from jax.sharding import PartitionSpec as P

bf16, f32 = jnp.bfloat16, jnp.float32
BY_AXES = pl.DeviceIdType.MESH
NN, NT, TN = ((1,), (0,)), ((1,), (1,)), ((0,), (0,))
UNIT = 256
PAIR = 2 * UNIT
PLANE = 4, 4
ALL = pl.ds(0, 4)
HALVES = pl.ds(0, 2), pl.ds(2, 2)
EPS = 1e-6


def dot(a, b, how):
    return lax.dot_general(a, b, (how, ((), ())), preferred_element_type=f32)


def sizes(x_shape, gate_shape, down_shape):
    s = types.SimpleNamespace()
    s.layers, s.rows, _ = gate_shape
    s.tokens, s.d = x_shape[1:]
    s.block = down_shape[1]
    s.padded = -(-s.block // 16) * 16
    s.ff = 16 * s.padded
    s.units = s.ff // UNIT
    s.sub = UNIT // 16
    s.early = -(-s.units // 2)
    s.late = s.units - s.early
    s.pair = 2 * s.rows
    s.both, s.wide, s.tile, s.half = 2 * s.tokens, 2 * s.ff, s.tokens // 4, s.d // 2
    return s


def here():
    return {name: lax.axis_index(name) for name in ("x", "y", "z", "c")}


def ring(v, k):
    return lax.rem(v + k + 4, 4)


def flip(v):
    return lax.rem(v, 2)


def greet(partners):
    barrier = pltpu.get_barrier_semaphore()
    for one in partners:
        pl.semaphore_signal(barrier, inc=1, device_id=one, device_id_type=BY_AXES)
    pl.semaphore_wait(barrier, len(partners))


def in_plane(me):
    return [{axis: ring(me[axis], k)} for axis in ("y", "z") for k in (1, -1)]


def beside(me):
    n = lax.axis_size("x")
    return [{"x": lax.rem(me["x"] + k, n)} for k in (1, n - 1)]


def twin(me):
    return {"c": 1 - me["c"]}


def remote(src, dst, sent, got, to):
    return pltpu.make_async_remote_copy(src_ref=src, dst_ref=dst, send_sem=sent, recv_sem=got, device_id=to, device_id_type=BY_AXES)


class Gather:
    def __init__(self, me, slot, sent, got, a, b):
        self.me, self.slot, self.sent, self.got, self.a, self.b = me, slot, sent, got, a, b

    def copy(self, u, m):
        i, j, x = self.me[self.a], self.me[self.b], self.me["x"]
        turn = 1 - 2 * flip(u)
        way = 1 - 2 * flip(u + x)
        came = ring(j, -way)
        if m < 2:
            at, to = (i, j), {self.a: ring(i, 1 - 2 * m)}
        elif m == 2:
            at, to = (ring(i, -turn), j), {self.a: ring(i, turn)}
        elif m == 3:
            at, to = (ALL, j), {self.b: ring(j, way)}
        elif m == 4:
            at, to = (ALL, came), {self.b: ring(j, way)}
        else:
            at, to = (pl.ds(2 * m - 10, 2), came), beside(self.me)[m - 5]
        ref = self.slot(u, *(at if self.a == "y" else at[::-1]))
        return remote(ref, ref, self.sent.at[u, m], self.got.at[u, m], to)

    def stage(self, k, u):
        for m in ((), (0, 1), (2,), (3,), (4, 5, 6))[k]:
            self.copy(u, m).wait_recv()
        for m in ((0, 1), (2,), (3,), (4, 5, 6), ())[k]:
            self.copy(u, m).start()
        if k == 4:
            for m in range(7):
                self.copy(u, m).wait_send()


def gather_sems(units):
    return [pltpu.SemaphoreType.DMA((units, 7)) for _ in range(8)]


DEPTH = 4


STAGES = 7


class Scatter:
    def __init__(self, me, bufs, sent, got, a, b):
        self.me, self.sent, self.got, self.a, self.b = me, sent, got, a, b
        self.term, self.rm, self.sm, self.r0, self.r1, self.t, self.q, self.s0, self.s1, self.x0, self.x1, self.tb, self.z0, self.z1 = bufs

    @staticmethod
    def scratch(rows, cols, units):
        sizes = [(3, 4, 4), (3, 4), (DEPTH,)] + [(2, 4)] * 4 + [(2,)] * 7
        return [pltpu.VMEM((*size, rows, cols), bf16) for size in sizes] + [pltpu.SemaphoreType.DMA((units, 11))] * 2

    def group(self, u, i, part=ALL):
        at = (i, part) if self.a == "y" else (part, i)
        return self.term.at[(lax.rem(u, 3), *at)]

    def copy(self, u, m):
        i, j, x = self.me[self.a], self.me[self.b], self.me["x"]
        turn, two, far = 1 - 2 * flip(u), flip(u), lax.rem(u, DEPTH)
        sems = self.sent.at[u, m], self.got.at[u, m]
        if m < 6:
            h, way = m % 2, 1 - 2 * (m % 2)
            same, other = HALVES[h], HALVES[1 - h]
            src, dst = ((self.group(u, ring(i, 2), same), self.r0.at[two, same]), (self.group(u, ring(i, way), other), self.rm.at[lax.rem(u, 3), other]), (self.t.at[two, same], self.r1.at[two, same]))[m // 2]
            return remote(src, dst, *sems, {self.a: ring(i, way)})
        if m < 9:
            src, dst, way = ((self.q.at[two, ring(j, 2)], self.s0.at[two], turn), (self.q.at[two, ring(j, -turn)], self.sm.at[far], -turn), (self.tb.at[two], self.s1.at[two], turn))[m - 6]
            return remote(src, dst, *sems, {self.b: ring(j, way)})
        src, dst = ((self.z0, self.x0), (self.z1, self.x1))[m - 9]
        way = (1 - 2 * flip(x)) * (1 if (self.a == "y") == (m == 9) else -1)
        return remote(src.at[two], dst.at[two], *sems, {"x": ring(x, way)})

    def start(self, u, m):
        for one in m:
            self.copy(u, one).start()

    def stage(self, k, u, put=None):
        i, j = self.me[self.a], self.me[self.b]
        turn, two, far = 1 - 2 * flip(u), flip(u), lax.rem(u, DEPTH)
        near, spread, last = range(6), range(6, 9), range(9, 11)
        for m in ((), near[:2], near[2:], spread[:1], spread[1:], last[:1], last[1:])[k]:
            self.copy(u, m).wait_recv()
        for m in ((), (), near, (), spread, last[:1], last[1:])[k]:
            self.copy(u, m).wait_send()
        wide = lambda ref, *at: ref[at].astype(f32)
        if k == 1:
            for half, way in zip(HALVES, (1, -1), strict=True):
                self.t[two, half] = (self.group(u, ring(i, way), half)[...].astype(f32) + wide(self.r0, two, half)).astype(bf16)
        if k == 2:
            self.q[two] = (self.group(u, i)[...].astype(f32) + wide(self.r1, two) + wide(self.rm, lax.rem(u, 3))).astype(bf16)
        if k == 3:
            self.tb[two] = (wide(self.q, two, ring(j, turn)) + wide(self.s0, two)).astype(bf16)
        if k == 4:
            self.z0[two] = (wide(self.q, two, j) + wide(self.s1, two) + wide(self.sm, far)).astype(bf16)
        if k == 5:
            self.z1[two] = (wide(self.z0, two) + wide(self.x0, two)).astype(bf16)
        if k == 6:
            put(u, wide(self.z1, two) + wide(self.x1, two))
        self.start(u, ((), near[4:], spread[:2], spread[2:], last[:1], last[1:], ())[k])


def call(kernel, name, number, **kw):
    params = dict(vmem_limit_bytes=67043328)
    if number is not None:
        params |= dict(collective_id=number, has_side_effects=True)
    return pl.pallas_call(kernel, name=name, compiler_params=pltpu.CompilerParams(**params), **kw)


ANY = pl.BlockSpec(memory_space=pl.ANY)


def whole(shape):
    return pl.BlockSpec(shape, lambda *_: (0,) * len(shape), pipeline_mode=pl.Buffered(1))


AXES = ("y", "z"), ("z", "y")
HALF = UNIT // 2


def streams_of(me, s, gates, downs, sems):
    out = []
    for buf, width in ((gates, UNIT), (downs, s.half)):
        for n, axes in enumerate(AXES):
            slot = lambda u, y, z, buf=buf, lanes=pl.ds(n * width, width): buf.at[u, y, z, :, lanes]
            out.append(Gather(me, slot, *sems[2 * len(out) : 2 * len(out) + 2], *axes))
    return out


def early(streams, units, stages):
    for k, u in stages:
        at_stage(streams, k, jnp.int32(u), units)


def at_stage(streams, k, u, units):
    @pl.when((u >= 0) & (u < units))
    def _():
        for stream in streams:
            stream.stage(k, u)


def silu_parts(gate):
    s = jax.nn.sigmoid(gate)
    return s, gate * s


def tiles(value, width, moves):
    lane = lax.broadcasted_iota(jnp.int32, (value.shape[0], HALF), 1)
    out = [jnp.zeros((value.shape[0], HALF), value.dtype)] * (width // HALF)
    for to, n, start in moves:
        for k in range(to // HALF, (to + n - 1) // HALF + 1):
            base = k * HALF - to
            low, high = max(start + base, 0), min(start + base + HALF, value.shape[1])
            piece = value[:, low:high]
            if high - low < HALF:
                gap = jnp.zeros((value.shape[0], HALF - (high - low)), value.dtype)
                piece = jnp.concatenate([gap, piece] if low > start + base else [piece, gap], 1)
            out[k] = jnp.where((lane >= -base) & (lane < n - base), piece, out[k])
    return out


def places(s, core):
    for u in range(s.units):
        for q in range(16):
            n = min(s.sub, s.block - u * s.sub)
            if n > 0:
                yield u * UNIT + q * s.sub, n, (2 * q + core) * s.block + u * s.sub


def prepare_kernel(s, wg, wu, wd, gates, downs, halves, padded, sems):
    me = here()
    greet([twin(me)])
    for layer in range(s.layers):
        for mat, w in enumerate((wg, wu)):
            for core in range(2):
                for k, tile in enumerate(tiles(w[layer].astype(f32), s.ff, places(s, core))):
                    halves[core, layer, k // 2, :, pl.ds(mat * UNIT + k % 2 * HALF, HALF)] = tile.astype(bf16)
        padded[layer] = jnp.concatenate([wd[:, layer], jnp.zeros((s.padded - s.block, s.d), bf16)], 0)
    c = me["c"]
    give = remote(halves.at[1 - c], gates.at[:, :, c], sems.at[0], sems.at[1], twin(me))
    keep = pltpu.make_async_copy(halves.at[c], gates.at[:, :, c], sems.at[2])
    rest = pltpu.make_async_copy(padded, downs, sems.at[3])
    for one in (give, keep, rest):
        one.start()
    for one in (give, keep, rest):
        one.wait()


VMEM = pl.BlockSpec(memory_space=pltpu.VMEM)


def array(*shape, dtype=bf16):
    return jax.ShapeDtypeStruct(shape, dtype)


def prepare(s, weights):
    half, down = (s.layers, s.units, s.rows, PAIR), (s.layers, s.padded, s.d)
    return call(
        functools.partial(prepare_kernel, s),
        "prepare",
        8,
        in_specs=[VMEM] * 3,
        out_specs=[ANY] * 2,
        out_shape=[array(s.layers, s.units, 2, s.rows, PAIR), array(*down)],
        scratch_shapes=[pltpu.VMEM((2, *half), bf16), pltpu.VMEM(down, bf16), pltpu.SemaphoreType.DMA((4,))],
    )(*weights)


WARM = [(k, d - k) for d in range(4) for k in range(d + 1)]


def parts(s):
    tile = s.tokens // 2
    return [pl.ds(n * tile, tile) for n in range(4)]


def lanes_of(u, width=UNIT):
    return pl.ds(pl.multiple_of(u * width, width), width)


def split(s, me, src, dst, u, width, sems):
    keep = pltpu.make_async_copy(src.at[pl.ds(0, s.tokens)], dst.at[:, lanes_of(u, width)], sems.at[0, u])
    give = remote(src.at[pl.ds(s.tokens, s.tokens)], dst.at[:, lanes_of(s.units + u, width)], sems.at[1, u], sems.at[2, u], twin(me))
    return keep, give


def first_kernel(s, x, dy, w, wd, acts, dys, gu, prod, downs, xv, av, pv, buf, dbuf, local, pair, prods, shared, *sems):
    me = here()
    j = pl.program_id(0)
    streams = streams_of(me, s, buf, dbuf, sems)
    y, z = me["y"], me["z"]
    rows = s.tile
    own_part = [pl.ds(n * rows, rows) for n in range(4)]

    def act_out(h):
        return pltpu.make_async_copy(av.at[pl.ds(h * s.tokens, s.tokens)], acts.at[h], local.at[5 + h])

    def share(n):
        return remote(av.at[own_part[n]], av.at[pl.ds(s.tokens + n * rows, rows)], pair.at[0, n], pair.at[1, n], twin(me))

    def prod_out(u):
        return split(s, me, pv.at[flip(u)], prod, u, UNIT, prods)

    def down_out(u):
        give = remote(dbuf.at[u], downs.at[1, u], shared.at[0, u], shared.at[1, u], twin(me))
        return pltpu.make_async_copy(dbuf.at[u], downs.at[0, u], shared.at[2, u]), give

    keep = pltpu.make_async_copy(xv.at[1], dys.at[0], local.at[4])
    give = remote(xv.at[1], dys.at[1], pair.at[0, 4], pair.at[1, 4], twin(me))

    @pl.when(j == 0)
    def _():
        own = [pltpu.make_async_copy(src.at[0], dst.at[:, y, z], local.at[n]) for n, (src, dst) in enumerate(((w, buf), (wd, dbuf)))]
        own += [pltpu.make_async_copy(one, xv.at[n], local.at[2 + n]) for n, one in enumerate((x, dy))]
        for one in own:
            one.start()
        greet(in_plane(me) + beside(me) + [twin(me)])
        own[0].wait()
        own[1].wait()
        early(streams, s.units, WARM[:3])
        own[2].wait()
        for n in range(4):
            wide = xv[0, own_part[n]].astype(f32)
            scale = lax.rsqrt(jnp.mean(wide * wide, -1, keepdims=True) + EPS)
            av[own_part[n]] = (wide * scale).astype(bf16)
            share(n).start()
            early(streams, s.units, WARM[3 + n : 4 + n])
        act_out(0).start()
        own[3].wait()
        keep.start()
        give.start()
        early(streams, s.units, WARM[7:])
        for n in range(4):
            share(n).wait()
        act_out(1).start()

    for k in range(5):
        at_stage(streams, 4 - k, j + k, s.units)
    for one in down_out(j):
        one.start()

    @pl.when(j >= 2)
    def _():
        for one in prod_out(j - 2):
            one.wait()

    weights = buf[j].reshape(s.d, PAIR)
    for part in parts(s):
        both = dot(av[part], weights, NN)
        gu[part] = both
        pv[flip(j), part] = (silu_parts(both[:, :UNIT])[1] * both[:, UNIT:]).astype(bf16)
    for one in prod_out(j):
        one.start()

    @pl.when(j == s.units - 1)
    def _():
        for one in (keep, give, act_out(0), act_out(1), *prod_out(j - 1), *prod_out(j)):
            one.wait()
        for u in range(s.units):
            for one in down_out(u):
                one.wait()


def first(s, x, dy, w, wd):
    both = (2, s.tokens, s.d)
    return call(
        functools.partial(first_kernel, s),
        "first",
        0,
        grid=(s.units,),
        in_specs=[ANY] * 4,
        out_specs=[ANY, ANY, pl.BlockSpec((s.both, PAIR), lambda j: (0, j)), ANY, ANY],
        out_shape=[array(*both), array(*both), array(s.both, s.wide, dtype=f32), array(s.tokens, s.wide), array(2, s.units, *PLANE, s.sub, s.d)],
        scratch_shapes=[
            pltpu.VMEM(both, bf16),
            pltpu.VMEM((s.both, s.d), bf16),
            pltpu.VMEM((2, s.both, UNIT), bf16),
            pltpu.VMEM((s.units, *PLANE, s.pair, PAIR), bf16),
            pltpu.VMEM((s.units, *PLANE, s.sub, s.d), bf16),
            pltpu.SemaphoreType.DMA((7,)),
            pltpu.SemaphoreType.DMA((2, 5)),
            pltpu.SemaphoreType.DMA((3, s.units)),
            pltpu.SemaphoreType.DMA((3, s.units)),
            *gather_sems(s.units),
        ],
    )(x, dy, w, wd)


class Both:
    def __init__(self, me, made, out, sems):
        self.me, self.made, self.out, self.sems = me, made, out, sems

    def copies(self, t):
        rows = self.made.shape[1]
        part, src = pl.ds(pl.multiple_of(t * rows, rows), rows), self.made.at[flip(t)]
        return pltpu.make_async_copy(src, self.out.at[0, part], self.sems.at[0, t]), remote(src, self.out.at[1, part], self.sems.at[1, t], self.sems.at[2, t], twin(self.me))

    def put(self, t, value):
        @pl.when(t >= 2)
        def _():
            for one in self.copies(t - 2):
                one.wait()

        self.made[flip(t)] = value
        for one in self.copies(t):
            one.start()

        @pl.when(t == 3)
        def _():
            for one in self.copies(t - 1) + self.copies(t):
                one.wait()


def tile_spec(s, width):
    return pl.BlockSpec((s.tile, width), lambda t: (t, 0))


def down_kernel(s, prod, w, h, wg, wd, h_out, acts, gates, downs, wv, total, gv, dv, local, saved, made, sent, *sems):
    me = here()
    t = pl.program_id(0)
    streams = streams_of(me, s, gv, dv, sems)
    loads = [pltpu.make_async_copy(w.at[n], wv.at[n], local.at[n]) for n in range(2)]

    @pl.when(t == 0)
    def _():
        y, z = me["y"], me["z"]
        own = [pltpu.make_async_copy(src.at[1, pl.ds(0, s.early)], dst.at[:, y, z], local.at[2 + n]) for n, (src, dst) in enumerate(((wg, gv), (wd, dv)))]
        for one in own + loads:
            one.start()
        greet(in_plane(me) + beside(me) + [twin(me)])
        for one in own:
            one.wait()

    def out(u):
        return [pltpu.make_async_copy(src.at[u], dst.at[u], saved.at[n, u]) for n, (src, dst) in enumerate(((gv, gates), (dv, downs)))]

    def slot(n):
        for k in reversed(range(5)):
            at_stage(streams, k, n - k, s.early)

        @pl.when((n >= 4) & (n < 4 + s.early))
        def _():
            for one in out(n - 4):
                one.start()

    slot(2 * t)

    @pl.when(t == 0)
    def _():
        loads[0].wait()

    total[...] = dot(prod[:, : s.ff], wv[0], NN)
    slot(2 * t + 1)

    @pl.when(t == 0)
    def _():
        loads[1].wait()

    y = (total[...] + dot(prod[:, s.ff :], wv[1], NN)).astype(bf16)
    new = (h[...].astype(f32) + y.astype(f32)).astype(bf16)
    h_out[...] = new
    wide = new.astype(f32)
    scale = lax.rsqrt(jnp.mean(wide * wide, -1, keepdims=True) + EPS)
    Both(me, made, acts, sent).put(t, (wide * scale).astype(bf16))

    @pl.when(t == 3)
    def _():
        slot(2 * t + 2)
        for u in range(s.early):
            for one in out(u):
                one.wait()


def own_rows(s):
    return [pltpu.VMEM((2, s.tile, s.d), bf16), pltpu.SemaphoreType.DMA((3, 4))]


def down(s, prod, w, h, wg, wd):
    tile = s.tile
    return call(
        functools.partial(down_kernel, s),
        "down",
        1,
        grid=(4,),
        in_specs=[tile_spec(s, s.wide), ANY, tile_spec(s, s.d), ANY, ANY],
        out_specs=[tile_spec(s, s.d), ANY, ANY, ANY],
        out_shape=[array(s.tokens, s.d), array(2, s.tokens, s.d), array(s.early, *PLANE, s.pair, PAIR), array(s.early, *PLANE, s.sub, s.d)],
        scratch_shapes=[
            pltpu.VMEM((2, s.ff, s.d), bf16),
            pltpu.VMEM((tile, s.d), f32),
            pltpu.VMEM((s.early, *PLANE, s.pair, PAIR), bf16),
            pltpu.VMEM((s.early, *PLANE, s.sub, s.d), bf16),
            pltpu.SemaphoreType.DMA((4,)),
            pltpu.SemaphoreType.DMA((2, s.early)),
            *own_rows(s),
            *gather_sems(s.early),
        ],
    )(prod, w, h, wg, wd)


def back_kernel(s, dgu, w0, w1, w2, h, by, out, wv, total, local, made, sent):
    me = here()
    t = pl.program_id(0)
    units = [w.at[u] for w in (w0, w1, w2) for u in range(w.shape[0])]
    loads = [pltpu.make_async_copy(one, wv.at[n // s.units, :, lanes_of(n % s.units, PAIR)], local.at[n]) for n, one in enumerate(units)]

    @pl.when(t == 0)
    def _():
        for load in loads:
            load.start()
        greet([twin(me)])
        for load in loads[: s.units]:
            load.wait()

    total[...] = dot(dgu[:, : s.wide], wv[0], NT)

    @pl.when(t == 0)
    def _():
        for load in loads[s.units :]:
            load.wait()

    da = (total[...] + dot(dgu[:, s.wide :], wv[1], NT)).astype(bf16).astype(f32)
    wide = h[...].astype(f32)
    scale = lax.rsqrt(jnp.mean(wide * wide, -1, keepdims=True) + EPS)
    along = jnp.mean(da * wide, -1, keepdims=True)
    dh = (scale * da - wide * (scale * scale * scale * along)).astype(bf16)
    Both(me, made, out, sent).put(t, (by[...].astype(f32) + dh.astype(f32)).astype(bf16))


def back(s, dgu, w0, w1, w2, h, by):
    return call(
        functools.partial(back_kernel, s),
        "back",
        2,
        grid=(4,),
        in_specs=[tile_spec(s, 2 * s.wide), ANY, ANY, ANY, tile_spec(s, s.d), tile_spec(s, s.d)],
        out_specs=ANY,
        out_shape=array(2, s.tokens, s.d),
        scratch_shapes=[pltpu.VMEM((2, s.d, s.wide), bf16), pltpu.VMEM((s.tile, s.d), f32), pltpu.SemaphoreType.DMA((2 * s.units,)), *own_rows(s)],
    )(dgu, w0, w1, w2, h, by)


def terms_scratch(s):
    return Scatter.scratch(s.pair, UNIT, s.units) * 2 + Scatter.scratch(s.sub, s.half, s.units) * 2


class Terms:
    def __init__(self, s, me, gates, downs, refs):
        self.s, self.gates, self.downs = s, gates, downs
        each = len(refs) // 4
        self.streams = [Scatter(me, refs[n * each : n * each + each - 2], *refs[n * each + each - 2 : n * each + each], *AXES[1 - n % 2]) for n in range(4)]

    def make(self, u, acts, dgu, prod, by):
        s, slot = self.s, lax.rem(u, 3)
        down = dot(prod[...], by[...], TN).astype(bf16)
        for n in range(2):
            self.streams[2 + n].term[slot] = down[:, n * s.half : (n + 1) * s.half].reshape(*PLANE, s.sub, s.half)
        for k in range(2):
            both = dot(acts[:, k * s.half : (k + 1) * s.half], dgu[...], TN).astype(bf16)
            for n in range(2):
                self.streams[n].term[slot, HALVES[k]] = both[:, n * UNIT : (n + 1) * UNIT].reshape(2, 4, s.pair, UNIT)

    def put(self, n, u, value):
        s = self.s
        if n < 2:
            self.gates[u, :, :, pl.ds(n * UNIT, UNIT)] = value.reshape(2, s.rows, UNIT).astype(bf16)
        else:
            self.downs[u, :, pl.ds((n - 2) * (s.half), s.half)] = value.astype(bf16)

    def settle(self, j):
        for k in reversed(range(STAGES)):
            u = j - k

            @pl.when((u >= 0) & (u < self.s.units))
            def _(k=k, u=u):
                for m in ((0, 1), (2, 3)) if k == 0 else ():
                    for stream in self.streams:
                        stream.start(u, m)
                for n, stream in enumerate(self.streams if k else ()):
                    stream.stage(k, u, functools.partial(self.put, n))


def sums(s):
    return [array(s.units, 2, s.rows, PAIR), array(s.units, s.sub, s.d)]


def arrivals(s, sources, targets, sems):
    return [[pltpu.make_async_copy(src.at[part], dst.at[part], sems.at[n, m]) for m, (src, dst) in enumerate(zip(sources, targets, strict=True))] for n, part in enumerate(parts(s))]


def wait_first(j, arrive):
    @pl.when(j == 0)
    def _():
        for one in sum(arrive, []):
            one.wait()


def back_gates(both, by):
    gate, up, by = both[:, :UNIT], both[:, UNIT:], by.astype(f32)
    sig, act = silu_parts(gate)
    return (by * up * (sig + act * (1.0 - sig))).astype(bf16), (by * act).astype(bf16), (act * up).astype(bf16)


def second_kernel(s, acts_in, dys_in, wg, wd, g_early, d_early, dgux, g_late, theirs, out_g, out_d, acts, dys, gv, dv, dgu, prod, tiles_in, local, saved, given, sent, *refs):
    me = here()
    j = pl.program_id(0)
    streams = streams_of(me, s, gv.at[pl.ds(2, s.late)], dv.at[pl.ds(2, s.late)], refs[:8])
    terms = Terms(s, me, out_g, out_d, refs[8:])

    def at(k, u):
        at_stage(streams, k, u, s.late)

    def load(u):
        return [pltpu.make_async_copy(src.at[u], dst.at[flip(u)], local.at[n, flip(u)]) for n, (src, dst) in enumerate(((g_early, gv), (d_early, dv)))]

    arrive = arrivals(s, (acts_in, dys_in), (acts, dys), tiles_in)

    def place(u):
        return jnp.where(u < s.early, flip(u), u - s.early + 2)

    def save(u):
        return pltpu.make_async_copy(gv.at[place(u)], g_late.at[u - s.early], saved)

    def give(u):
        return remote(gv.at[place(u)], theirs.at[u], given.at[0, u], given.at[1, u], twin(me))

    def dgu_out(u):
        return split(s, me, dgu, dgux, u, PAIR, sent)

    @pl.when(j == 0)
    def _():
        y, z = me["y"], me["z"]
        rest = pl.ds(s.early, s.late)
        own = [pltpu.make_async_copy(src.at[1, rest], dst.at[pl.ds(2, s.late), y, z], local.at[2, n]) for n, (src, dst) in enumerate(((wg, gv), (wd, dv)))]
        for one in own + load(0) + load(1) + sum(arrive, []):
            one.start()
        greet(in_plane(me) + beside(me) + [twin(me)])
        for one in own:
            one.wait()

    for k in reversed(range(5)):
        at(k, j - k)

    @pl.when((j >= 1) & (j <= s.units))
    def _():
        for one in (*dgu_out(j - 1), give(j - 1)):
            one.wait()

    @pl.when((j > s.early) & (j <= s.units))
    def _():
        save(j - 1).wait()

    @pl.when(j < s.units)
    def _():
        @pl.when(j < s.early)
        def _():
            for one in load(j):
                one.wait()

        @pl.when((j >= 1) & (j + 1 < s.early))
        def _():
            for one in load(j + 1):
                one.start()

        @pl.when(j >= s.early)
        def _():
            save(j).start()

        give(j).start()
        wait_first(j, arrive)
        now = place(j)
        weights, ahead = gv[now].reshape(s.d, PAIR), dv[now].reshape(UNIT, s.d)
        for part in parts(s):
            both = dot(acts[part], weights, NN)
            by = dot(dys[part], ahead, NT).astype(bf16)
            dgu[part, :UNIT], dgu[part, UNIT:], prod[part] = back_gates(both, by)
        for one in dgu_out(j):
            one.start()
        terms.make(j, acts, dgu, prod, dys)

    terms.settle(j)


def second(s, acts, dys, wg, wd, g_early, d_early):
    unit, row = (*PLANE, s.pair, PAIR), (*PLANE, s.sub, s.d)
    return call(
        functools.partial(second_kernel, s),
        "second",
        3,
        grid=(s.units + STAGES - 1,),
        in_specs=[ANY] * 6,
        out_specs=[ANY] * 3 + [whole(one.shape) for one in sums(s)],
        out_shape=[array(s.tokens, 2 * s.wide), array(s.late, *unit), array(s.units, *unit), *sums(s)],
        scratch_shapes=[
            *[pltpu.VMEM((s.both, s.d), bf16)] * 2,
            pltpu.VMEM((2 + s.late, *unit), bf16),
            pltpu.VMEM((2 + s.late, *row), bf16),
            pltpu.VMEM((s.both, PAIR), bf16),
            pltpu.VMEM((s.both, UNIT), bf16),
            pltpu.SemaphoreType.DMA((4, 2)),
            pltpu.SemaphoreType.DMA((3, 2)),
            pltpu.SemaphoreType.DMA,
            pltpu.SemaphoreType.DMA((2, s.units)),
            pltpu.SemaphoreType.DMA((3, s.units)),
            *gather_sems(s.late),
            *terms_scratch(s),
        ],
    )(acts, dys, wg, wd, g_early, d_early)


def third_kernel(s, acts_in, dh_in, wd, gu, out_g, out_d, acts, dh, dgu, prod, tiles_in, *refs):
    me = here()
    j = pl.program_id(0)
    terms = Terms(s, me, out_g, out_d, refs)
    arrive = arrivals(s, (dh_in, acts_in), (dh, acts), tiles_in)

    @pl.when(j == 0)
    def _():
        for one in sum(arrive, []):
            one.start()
        greet(in_plane(me) + beside(me))

    @pl.when(j < s.units)
    def _():
        wait_first(j, arrive)
        ahead = wd[...]
        for part in parts(s):
            by = dot(dh[part], ahead, NT).astype(bf16)
            dgu[part, :UNIT], dgu[part, UNIT:], prod[part] = back_gates(gu[part], by)
        terms.make(j, acts, dgu, prod, dh)

    terms.settle(j)


def third(s, number, acts, dh, wd, gu):
    at = lambda j: jnp.minimum(j, s.units - 1)
    return call(
        functools.partial(third_kernel, s),
        "third",
        number,
        grid=(s.units + STAGES - 1,),
        in_specs=[ANY] * 2 + [pl.BlockSpec((UNIT, s.d), lambda j: (at(j), 0)), pl.BlockSpec((s.both, PAIR), lambda j: (0, at(j)))],
        out_specs=[whole(one.shape) for one in sums(s)],
        out_shape=sums(s),
        scratch_shapes=[
            *[pltpu.VMEM((s.both, s.d), bf16)] * 2,
            pltpu.VMEM((s.both, PAIR), bf16),
            pltpu.VMEM((s.both, UNIT), bf16),
            pltpu.SemaphoreType.DMA((4, 2)),
            *terms_scratch(s),
        ],
    )(acts, dh, wd, gu)


def adamw(w, m, v, g):
    m = 0.9 * m + 0.1 * g
    v = 0.95 * v + 0.05 * g * g
    step = m * lax.rsqrt(v + 1e-8) + 0.1 * w
    return (w - 0.02 * step).astype(bf16), m, v


def total_kernel(g0, d0, g1, d1, got, out, sums, sent, here_got):
    me = here()
    greet(in_plane(me) + [{axis: ring(me[axis], 2)} for axis in ("y", "z")] + [twin(me)])
    pairs = [remote(g.at[:, 1 - me["c"]], got.at[n], sent.at[n], here_got.at[n], twin(me)) for n, g in enumerate((g0, g1))]
    for one in pairs:
        one.start()
    total = sum(jnp.sum(g[...].astype(f32) ** 2) for g in (g0, d0, g1, d1))
    total = jnp.full(out.shape, total)
    base = 0
    for axis in "cyz":
        size = lax.axis_size(axis)
        sums[base] = total
        copies = []
        for k in range(1, size):
            to = {axis: lax.rem(me[axis] + k, size)}
            copies.append(remote(sums.at[base], sums.at[base + k], sent.at[base + k + 1], here_got.at[base + k + 1], to))
            copies[-1].start()
        for k, one in enumerate(copies):
            one.wait()
            total += sums[base + k + 1]
        base += size
    out[...] = total
    for one in pairs:
        one.wait()


def total(number, *sums):
    tile, shape = (8, HALF), sums[0].shape
    sems = pltpu.SemaphoreType.DMA((12,))
    return call(
        total_kernel,
        "total",
        number,
        in_specs=[VMEM] * 4,
        out_specs=[VMEM] * 2,
        out_shape=[array(2, shape[0], *shape[2:]), array(*tile, dtype=f32)],
        scratch_shapes=[pltpu.VMEM((10, *tile), f32), sems, sems],
    )(*sums)


def finish_kernel(s, g0, d0, g1, d1, got, squares, *refs):
    old, new = refs[:9], refs[9:]
    c = lax.axis_index("c")
    count = 16 * (s.layers * s.pair * 32 * s.block * 3)
    factor = jnp.minimum(1.0, 0.5 * lax.rsqrt(squares[:1, :1] / count + 1e-30))
    moves = [(start, n, core * s.ff + to) for core in range(2) for to, n, start in places(s, core)]

    def update(n, at, g):
        w, m, v = (old[n + 3 * k] for k in range(3))
        made = adamw(w[at].astype(f32), m[at], v[at], g * factor)
        for k, value in enumerate(made):
            new[n + 3 * k][at] = value

    for layer, (g, d) in enumerate(((g0, d0), (g1, d1))):
        for mat in range(2):
            lanes = pl.ds(mat * UNIT, UNIT)
            pieces = [[ref[u, c, :, lanes] if ref is g else ref[layer, u, :, lanes] for u in range(s.units)] for ref in (g, got)]
            mine, other = (jnp.concatenate(piece, 1).astype(f32) for piece in pieces)
            both = jnp.concatenate([jnp.where(c == 0, mine, other), jnp.where(c == 0, other, mine)], 1)
            update(mat, layer, jnp.concatenate(tiles(both, 32 * s.block, moves), 1))
        update(2, (slice(None), layer), d[...].astype(f32).reshape(s.padded, s.d)[: s.block])


def finish(s, sums, got, squares, old):
    out = [array(*one.shape, dtype=one.dtype) for one in old]
    return call(functools.partial(finish_kernel, s), "finish", None, in_specs=[VMEM] * 15, out_specs=[VMEM] * 9, out_shape=out)(*sums, got, squares, *old)


def turned(arrays):
    return [one.swapaxes(0, 1) if n % 3 == 2 else one for n, one in enumerate(arrays)]


def solution(mesh):
    cut_mesh = Mesh(mesh.devices.reshape(mesh.shape["rep"], mesh.shape["r"], 4, 4, 2), ("rep", "x", "y", "z", "c"))

    def step(x, dy, *arrays):
        s = sizes(x.shape, arrays[0].shape, arrays[2].shape)
        arrays = turned(arrays)
        flat = (s.both, s.d)
        gates, downs = prepare(s, arrays[:3])
        gates = gates.reshape(s.layers, s.units, s.pair, PAIR)
        downs = downs.reshape(s.layers, s.units, s.sub, s.d)
        acts0, dys, gu0, prod0, wd0 = first(s, x[0], dy[0], gates, downs)
        h1, acts1, g_early, d_early = down(s, prod0, wd0.reshape(2, s.ff, s.d), x[0], gates, downs)
        dys, acts0, acts1 = (one.reshape(flat) for one in (dys, acts0, acts1))
        dgu1, g_late, theirs, *sums1 = second(s, acts1, dys, gates, downs, g_early, d_early)
        w = (one.reshape(-1, s.d, PAIR) for one in (g_early, g_late, theirs))
        dh = back(s, dgu1, *w, h1, dy[0]).reshape(flat)
        sums0 = third(s, 6, acts0, dh, wd0.reshape(-1, s.d), gu0)
        return tuple(turned(finish(s, (*sums0, *sums1), *total(7, *sums0, *sums1), arrays)))

    place = ("y", "z", "c")
    states, cut = P(("rep", "x", *place), None, None), P(None, place, None)
    return jax.shard_map(
        step,
        mesh=cut_mesh,
        in_specs=(states, states) + (cut,) * 9,
        out_specs=(P("rep", place, None),) * 9,
        check_vma=False,
    )
```

time: 1410 us -> 685 us (0.49)
  Pallas kernels: 0 us -> 683 us
  matrix products: 565 us -> 0 us
  waiting for transfers between devices: 532 us -> 0 us
  blocking collectives: 210 us -> 0 us
  local copies, waits for them, and re-layouts: 36 us -> 0 us
  other arithmetic: 28.8 us -> 0 us
  between operations: 17.9 us -> 0.96 us
    pallas_call x0 -> x8, Pallas kernels: none -> 683 us  [the longest x1 227 us: second(): call(functools.partial(second_kernel, s), 'second', 3, grid=(s.units + ST...]
    dot_general x15 -> x0, matrix products: 565 us -> none  [the longest x5 196 us: layer(): gate = jnp.dot(a, w['w_gate'], preferred_element_type=jnp.float32)]
    unnamed x17 -> x0, waiting for transfers between devices: 255 us -> none
    all_gather x6 -> x0, waiting for transfers between devices: 213 us -> none  [fetched(): lax.all_gather(w[number], 's', axis=0, tiled=True)]
    unnamed x1 -> x0, blocking collectives: 146 us -> none
    psum x1 -> x0, waiting for transfers between devices: 64 us -> none  [summed(): lax.psum(lax.psum_scatter(term, 's', scatter_dimension=0, tiled=True), 'r')]
    psum x1 -> x0, blocking collectives: 63.9 us -> none  [step(): squares = lax.psum(sum((jnp.sum(g * g) for g in gradients)), 's')]
    unnamed x42 -> x0, local copies, waits for them, and re-layouts: 26.6 us -> none
  transfers between devices with their start and end apart: 13 -> 0, of which waited for: 12 -> 0; matrix products, arithmetic and copies ran while one was open for 39% -> 0% of each run, Pallas kernels for 0% -> 0%
where the time goes in v1:
time: 685 us; the launch traced here: 684 us
  Pallas kernels  683 us (100%)
    pallas_call x1, Pallas kernels, second(): call(functools.partial(second_kernel, s), 'second', 3, grid=(s.units + ST...  227 us
    pallas_call x1, Pallas kernels, third(): call(functools.partial(third_kernel, s), 'third', number, grid=(s.units +...  156 us
    pallas_call x1, Pallas kernels, first(): call(functools.partial(first_kernel, s), 'first', 0, grid=(s.units,), in_...  106 us
    pallas_call x1, Pallas kernels, back(): call(functools.partial(back_kernel, s), 'back', 2, grid=(4,), in_specs=[t...  81.6 us
    pallas_call x1, Pallas kernels, down(): call(functools.partial(down_kernel, s), 'down', 1, grid=(4,), in_specs=[t...  66.3 us
    pallas_call x1, Pallas kernels, finish(): call(functools.partial(finish_kernel, s), 'finish', None, in_specs=[VMEM]...  18.2 us
    pallas_call x1, Pallas kernels, total(): call(total_kernel, 'total', number, in_specs=[VMEM] * 4, out_specs=[VMEM]...  15.5 us

profile of v1, /device:TPU:1, one launch (start us, length us, event | category | flops | bytes accessed | tf_op | source)
XLA Modules:
  0.0 684.2 jit_solution(642719440492346773)
XLA Ops:
  0.6 12.4 %prepare.1 = (bf16[2,9,2,40,512]{4,3,2,1,0:T(8,128)(2,1)}, bf16[2,144,1280]{2,1,0:T(8,128)(2,1)}) custom-call(bf16[2,40,4480]{2,1,0:T(8,128)(2,1)} %refs_0_.1, bf16[2,40,4480]{2,1,0:T(8,128)(2,1)} %refs_1_.1, bf16[140,2,1280]{2,1,0:T(2,128)(2,1)} %bitcast.38), custom_call_target="tpu_custom_call" | custom-call | tf_op jit(solution)/shard_map/prepare/pallas_call | solution.py:275
  13.1 106.4 %first.1 = (bf16[2,2048,1280]{2,1,0:T(8,128)(2,1)}, bf16[2,2048,1280]{2,1,0:T(8,128)(2,1)}, f32[4096,4608]{1,0:T(8,128)}, bf16[2048,4608]{1,0:T(8,128)(2,1)}, bf16[2,9,4,4,16,1280]{5,4,3,2,1,0:T(8,128)(2,1)}) custom-call(bf16[2048,1280]{1,0:T(8,128)(2,1)} %bitcast.25, bf16[2048,1280]{1,0:T(8,128)(2,1)} %bitcast.23, bf16[2,9,80,512]{3,2,1,0:T(8,128)(2,1)} %bitcast.27, ...), custom_call_target="tpu_custom_call" | custom-call | tf_op jit(solution)/shard_map/first/pallas_call | solution.py:383
  119.5 66.3 %down.1 = (bf16[2048,1280]{1,0:T(8,128)(2,1)}, bf16[2,2048,1280]{2,1,0:T(8,128)(2,1)}, bf16[5,4,4,80,512]{4,3,2,1,0:T(8,128)(2,1)}, bf16[5,4,4,16,1280]{4,3,2,1,0:T(8,128)(2,1)}) custom-call(bf16[2048,4608]{1,0:T(8,128)(2,1)} %get-tuple-element.41.prod, bf16[2,2304,1280]{2,1,0:T(8,128)(2,1)} %bitcast.19, bf16[2048,1280]{1,0:T(8,128)(2,1)} %bitcast.26, ...), custom_call_target="tpu_custom_call" | custom-call | tf_op jit(solution)/shard_map/down/pallas_call | solution.py:497
  185.8 227.2 %second.1 = (bf16[2048,9216]{1,0:T(8,128)(2,1)}, bf16[4,4,4,80,512]{4,3,2,1,0:T(8,128)(2,1)}, bf16[9,4,4,80,512]{4,3,2,1,0:T(8,128)(2,1)}, bf16[9,2,40,512]{3,2,1,0:T(8,128)(2,1)}, bf16[9,16,1280]{2,1,0:T(8,128)(2,1)}) custom-call(bf16[4096,1280]{1,0:T(8,128)(2,1)} %bitcast.33, bf16[4096,1280]{1,0:T(8,128)(2,1)} %bitcast.32, ...), custom_call_target="tpu_custom_call" | custom-call | tf_op jit(solution)/shard_map/second/pallas_call | solution.py:703
  413.0 81.6 %back.1 = bf16[2,2048,1280]{2,1,0:T(8,128)(2,1)} custom-call(bf16[2048,9216]{1,0:T(8,128)(2,1)} %get-tuple-element.47.dgu, bf16[5,1280,512]{2,1,0:T(8,128)(2,1)} %bitcast.22, bf16[4,1280,512]{2,1,0:T(8,128)(2,1)} %bitcast.37, bf16[9,1280,512]{2,1,0:T(8,128)(2,1)} %bitcast.30, bf16[2048,1280]{1,0:T(8,128)(2,1)} %get-tuple-element.50.h, ...), custom_call_target="tpu_custom_call" | custom-call | tf_op jit(solution)/shard_map/back/pallas_call | solution.py:548
  494.7 155.6 %third.1 = (bf16[9,2,40,512]{3,2,1,0:T(8,128)(2,1)}, bf16[9,16,1280]{2,1,0:T(8,128)(2,1)}) custom-call(bf16[4096,1280]{1,0:T(8,128)(2,1)} %bitcast.31, bf16[4096,1280]{1,0:T(8,128)(2,1)} %bitcast.21, bf16[4608,1280]{1,0:T(8,128)(2,1)} %bitcast.20, f32[4096,4608]{1,0:T(8,128)} %get-tuple-element.51.gu), custom_call_target="tpu_custom_call" | custom-call | tf_op jit(solution)/shard_map/third/pallas_call | solution.py:754
  650.3 15.5 %total.1 = (bf16[2,9,40,512]{3,2,1,0:T(8,128)(2,1)}, f32[8,128]{1,0:T(8,128)}) custom-call(bf16[9,2,40,512]{3,2,1,0:T(8,128)(2,1)} %get-tuple-element.52.g0, bf16[9,16,1280]{2,1,0:T(8,128)(2,1)} %get-tuple-element.53.d0, bf16[9,2,40,512]{3,2,1,0:T(8,128)(2,1)} %get-tuple-element.54.g1, bf16[9,16,1280]{2,1,0:T(8,128)(2,1)} %get-tuple-element.55.d1), custom_call_target="tpu_custom_call" | custom-call | tf_op jit(solution)/shard_map/total/pallas_call | solution.py:808
  665.8 18.2 %finish.1 = (bf16[2,40,4480]{2,1,0:T(8,128)(2,1)}, bf16[2,40,4480]{2,1,0:T(8,128)(2,1)}, bf16[140,2,1280]{2,1,0:T(2,128)(2,1)}, f32[2,40,4480]{2,1,0:T(8,128)}, ...) custom-call(bf16[9,2,40,512]{3,2,1,0:T(8,128)(2,1)} %get-tuple-eleme, ...), custom_call_target="tpu_custom_call" | custom-call | tf_op jit(solution)/shard_map/finish/pallas_call | solution.py:844

commit v2 on v1

--- a/solution.py
+++ b/solution.py
@@ -15,6 +15,7 @@
 UNIT = 256
 PAIR = 2 * UNIT
 PLANE = 4, 4
+TILES = 8
 ALL = pl.ds(0, 4)
 HALVES = pl.ds(0, 2), pl.ds(2, 2)
 EPS = 1e-6
@@ -33,10 +34,10 @@
     s.ff = 16 * s.padded
     s.units = s.ff // UNIT
     s.sub = UNIT // 16
-    s.early = -(-s.units // 2)
+    s.early = s.units // 3
     s.late = s.units - s.early
     s.pair = 2 * s.rows
-    s.both, s.wide, s.tile, s.half = 2 * s.tokens, 2 * s.ff, s.tokens // 4, s.d // 2
+    s.both, s.wide, s.tile, s.half = 2 * s.tokens, 2 * s.ff, s.tokens // TILES, s.d // 2
     return s
 
 
@@ -306,7 +307,7 @@
     j = pl.program_id(0)
     streams = streams_of(me, s, buf, dbuf, sems)
     y, z = me["y"], me["z"]
-    rows = s.tile
+    rows = s.tokens // 4
     own_part = [pl.ds(n * rows, rows) for n in range(4)]
 
     def act_out(h):
@@ -404,144 +405,149 @@
 
 
 class Both:
-    def __init__(self, me, made, out, sems):
-        self.me, self.made, self.out, self.sems = me, made, out, sems
+    def __init__(self, s, me, out, total, made, sems):
+        self.s, self.me, self.out, self.total, self.made, self.sems = s, me, out, total, made, sems
+
+    @staticmethod
+    def scratch(s):
+        return [pltpu.VMEM((s.tile, s.d), f32), pltpu.VMEM((2, s.tile, s.d), bf16), pltpu.SemaphoreType.DMA((3, TILES))]
 
     def copies(self, t):
-        rows = self.made.shape[1]
-        part, src = pl.ds(pl.multiple_of(t * rows, rows), rows), self.made.at[flip(t)]
-        return pltpu.make_async_copy(src, self.out.at[0, part], self.sems.at[0, t]), remote(src, self.out.at[1, part], self.sems.at[1, t], self.sems.at[2, t], twin(self.me))
-
-    def put(self, t, value):
-        @pl.when(t >= 2)
+        part, src = pl.ds(pl.multiple_of(t * self.s.tile, self.s.tile), self.s.tile), self.made.at[flip(t)]
+        keep = pltpu.make_async_copy(src, self.out.at[0, part], self.sems.at[0, t])
+        return keep, remote(src, self.out.at[1, part], self.sems.at[1, t], self.sems.at[2, t], twin(self.me))
+
+    def step(self, t, product, make):
+        @pl.when(t > 2)
         def _():
-            for one in self.copies(t - 2):
+            for one in self.copies(t - 3):
                 one.wait()
 
-        self.made[flip(t)] = value
-        for one in self.copies(t):
-            one.start()
-
-        @pl.when(t == 3)
+        def finish():
+            self.made[flip(t - 1)] = make(self.total[...])
+            for one in self.copies(t - 1):
+                one.start()
+
+        @pl.when((t > 0) & (t < TILES))
         def _():
-            for one in self.copies(t - 1) + self.copies(t):
+            finish()
+            self.total[...] = product()
+
+        @pl.when(t == TILES)
+        def _():
+            finish()
+            for one in self.copies(t - 2) + self.copies(t - 1):
                 one.wait()
 
 
-def tile_spec(s, width):
-    return pl.BlockSpec((s.tile, width), lambda t: (t, 0))
-
-
-def down_kernel(s, prod, w, h, wg, wd, h_out, acts, gates, downs, wv, total, gv, dv, local, saved, made, sent, *sems):
+def tile_spec(s, width, late):
+    return pl.BlockSpec((s.tile, width), lambda t: (jnp.clip(t - late, 0, TILES - 1), 0))
+
+
+def down_kernel(s, prod, w, h, wg, wd, h_out, acts, gates, downs, wv, gv, dv, local, saved, *refs):
     me = here()
     t = pl.program_id(0)
-    streams = streams_of(me, s, gv, dv, sems)
-    loads = [pltpu.make_async_copy(w.at[n], wv.at[n], local.at[n]) for n in range(2)]
+    both, streams = Both(s, me, acts, *refs[:3]), streams_of(me, s, gv, dv, refs[3:])
+    thirds = [pl.ds(n * s.wide // 3, s.wide // 3) for n in range(3)]
+
+    def out(u):
+        return [pltpu.make_async_copy(src.at[u], dst.at[u], saved.at[n, u]) for n, (src, dst) in enumerate(((gv, gates), (dv, downs)))]
+
+    def slot(n):
+        for k in reversed(range(5)):
+            at_stage(streams, k, n - 2 * k, s.early)
+
+        @pl.when((n >= TILES) & (n < TILES + s.early))
+        def _():
+            for one in out(n - TILES):
+                one.start()
 
     @pl.when(t == 0)
     def _():
-        y, z = me["y"], me["z"]
-        own = [pltpu.make_async_copy(src.at[1, pl.ds(0, s.early)], dst.at[:, y, z], local.at[2 + n]) for n, (src, dst) in enumerate(((wg, gv), (wd, dv)))]
+        loads = [pltpu.make_async_copy(w.at[part], wv.at[part], local.at[n]) for n, part in enumerate(thirds)]
+        own = [pltpu.make_async_copy(src.at[1, pl.ds(0, s.early)], dst.at[:, me["y"], me["z"]], local.at[3 + n]) for n, (src, dst) in enumerate(((wg, gv), (wd, dv)))]
         for one in own + loads:
             one.start()
         greet(in_plane(me) + beside(me) + [twin(me)])
         for one in own:
             one.wait()
-
-    def out(u):
-        return [pltpu.make_async_copy(src.at[u], dst.at[u], saved.at[n, u]) for n, (src, dst) in enumerate(((gv, gates), (dv, downs)))]
-
-    def slot(n):
-        for k in reversed(range(5)):
-            at_stage(streams, k, n - k, s.early)
-
-        @pl.when((n >= 4) & (n < 4 + s.early))
-        def _():
-            for one in out(n - 4):
-                one.start()
-
-    slot(2 * t)
-
-    @pl.when(t == 0)
-    def _():
-        loads[0].wait()
-
-    total[...] = dot(prod[:, : s.ff], wv[0], NN)
-    slot(2 * t + 1)
-
-    @pl.when(t == 0)
-    def _():
-        loads[1].wait()
-
-    y = (total[...] + dot(prod[:, s.ff :], wv[1], NN)).astype(bf16)
-    new = (h[...].astype(f32) + y.astype(f32)).astype(bf16)
-    h_out[...] = new
-    wide = new.astype(f32)
-    scale = lax.rsqrt(jnp.mean(wide * wide, -1, keepdims=True) + EPS)
-    Both(me, made, acts, sent).put(t, (wide * scale).astype(bf16))
-
-    @pl.when(t == 3)
-    def _():
-        slot(2 * t + 2)
+        for n, part in enumerate(thirds):
+            slot(jnp.int32(n))
+            loads[n].wait()
+            product = dot(prod[:, part], wv[part], NN)
+            both.total[...] = both.total[...] + product if n else product
+
+    @pl.when(t > 0)
+    def _():
+        slot(t + 2)
+
+    def make(total):
+        new = (h[...].astype(f32) + total.astype(bf16).astype(f32)).astype(bf16)
+        h_out[...] = new
+        wide = new.astype(f32)
+        scale = lax.rsqrt(jnp.mean(wide * wide, -1, keepdims=True) + EPS)
+        return (wide * scale).astype(bf16)
+
+    both.step(t, lambda: dot(prod[...], wv[...], NN), make)
+
+    @pl.when(t == TILES)
+    def _():
         for u in range(s.early):
             for one in out(u):
                 one.wait()
 
 
-def own_rows(s):
-    return [pltpu.VMEM((2, s.tile, s.d), bf16), pltpu.SemaphoreType.DMA((3, 4))]
-
-
 def down(s, prod, w, h, wg, wd):
-    tile = s.tile
+    unit, row = (s.early, *PLANE, s.pair, PAIR), (s.early, *PLANE, s.sub, s.d)
     return call(
         functools.partial(down_kernel, s),
         "down",
         1,
-        grid=(4,),
-        in_specs=[tile_spec(s, s.wide), ANY, tile_spec(s, s.d), ANY, ANY],
-        out_specs=[tile_spec(s, s.d), ANY, ANY, ANY],
-        out_shape=[array(s.tokens, s.d), array(2, s.tokens, s.d), array(s.early, *PLANE, s.pair, PAIR), array(s.early, *PLANE, s.sub, s.d)],
+        grid=(TILES + 1,),
+        in_specs=[tile_spec(s, s.wide, 0), ANY, tile_spec(s, s.d, 1), ANY, ANY],
+        out_specs=[tile_spec(s, s.d, 1), ANY, ANY, ANY],
+        out_shape=[array(s.tokens, s.d), array(2, s.tokens, s.d), array(*unit), array(*row)],
         scratch_shapes=[
-            pltpu.VMEM((2, s.ff, s.d), bf16),
-            pltpu.VMEM((tile, s.d), f32),
-            pltpu.VMEM((s.early, *PLANE, s.pair, PAIR), bf16),
-            pltpu.VMEM((s.early, *PLANE, s.sub, s.d), bf16),
-            pltpu.SemaphoreType.DMA((4,)),
+            pltpu.VMEM((s.wide, s.d), bf16),
+            pltpu.VMEM(unit, bf16),
+            pltpu.VMEM(row, bf16),
+            pltpu.SemaphoreType.DMA((5,)),
             pltpu.SemaphoreType.DMA((2, s.early)),
-            *own_rows(s),
+            *Both.scratch(s),
             *gather_sems(s.early),
         ],
     )(prod, w, h, wg, wd)
 
 
-def back_kernel(s, dgu, w0, w1, w2, h, by, out, wv, total, local, made, sent):
+def back_kernel(s, dgu, w0, w1, w2, h, by, out, wv, local, *refs):
     me = here()
     t = pl.program_id(0)
+    both = Both(s, me, out, *refs)
     units = [w.at[u] for w in (w0, w1, w2) for u in range(w.shape[0])]
-    loads = [pltpu.make_async_copy(one, wv.at[n // s.units, :, lanes_of(n % s.units, PAIR)], local.at[n]) for n, one in enumerate(units)]
 
     @pl.when(t == 0)
     def _():
+        loads = [pltpu.make_async_copy(one, wv.at[:, pl.ds(n * PAIR, PAIR)], local.at[n]) for n, one in enumerate(units)]
         for load in loads:
             load.start()
         greet([twin(me)])
-        for load in loads[: s.units]:
-            load.wait()
-
-    total[...] = dot(dgu[:, : s.wide], wv[0], NT)
-
-    @pl.when(t == 0)
-    def _():
-        for load in loads[s.units :]:
-            load.wait()
-
-    da = (total[...] + dot(dgu[:, s.wide :], wv[1], NT)).astype(bf16).astype(f32)
-    wide = h[...].astype(f32)
-    scale = lax.rsqrt(jnp.mean(wide * wide, -1, keepdims=True) + EPS)
-    along = jnp.mean(da * wide, -1, keepdims=True)
-    dh = (scale * da - wide * (scale * scale * scale * along)).astype(bf16)
-    Both(me, made, out, sent).put(t, (by[...].astype(f32) + dh.astype(f32)).astype(bf16))
+        each = len(units) // 3
+        for n in range(3):
+            for load in loads[n * each : (n + 1) * each]:
+                load.wait()
+            part = pl.ds(n * each * PAIR, each * PAIR)
+            product = dot(dgu[:, part], wv[:, part], NT)
+            both.total[...] = both.total[...] + product if n else product
+
+    def make(total):
+        da = total.astype(bf16).astype(f32)
+        wide = h[...].astype(f32)
+        scale = lax.rsqrt(jnp.mean(wide * wide, -1, keepdims=True) + EPS)
+        along = jnp.mean(da * wide, -1, keepdims=True)
+        dh = (scale * da - wide * (scale * scale * scale * along)).astype(bf16)
+        return (by[...].astype(f32) + dh.astype(f32)).astype(bf16)
+
+    both.step(t, lambda: dot(dgu[...], wv[...], NT), make)
 
 
 def back(s, dgu, w0, w1, w2, h, by):
@@ -549,11 +555,11 @@
         functools.partial(back_kernel, s),
         "back",
         2,
-        grid=(4,),
-        in_specs=[tile_spec(s, 2 * s.wide), ANY, ANY, ANY, tile_spec(s, s.d), tile_spec(s, s.d)],
+        grid=(TILES + 1,),
+        in_specs=[tile_spec(s, 2 * s.wide, 0), ANY, ANY, ANY, tile_spec(s, s.d, 1), tile_spec(s, s.d, 1)],
         out_specs=ANY,
         out_shape=array(2, s.tokens, s.d),
-        scratch_shapes=[pltpu.VMEM((2, s.d, s.wide), bf16), pltpu.VMEM((s.tile, s.d), f32), pltpu.SemaphoreType.DMA((2 * s.units,)), *own_rows(s)],
+        scratch_shapes=[pltpu.VMEM((s.d, 2 * s.wide), bf16), pltpu.SemaphoreType.DMA((2 * s.units,)), *Both.scratch(s)],
     )(dgu, w0, w1, w2, h, by)
 
 
@@ -567,11 +573,13 @@
         each = len(refs) // 4
         self.streams = [Scatter(me, refs[n * each : n * each + each - 2], *refs[n * each + each - 2 : n * each + each], *AXES[1 - n % 2]) for n in range(4)]
 
-    def make(self, u, acts, dgu, prod, by):
+    def make(self, u, acts, dgu, prod, by, between=()):
         s, slot = self.s, lax.rem(u, 3)
         down = dot(prod[...], by[...], TN).astype(bf16)
         for n in range(2):
             self.streams[2 + n].term[slot] = down[:, n * s.half : (n + 1) * s.half].reshape(*PLANE, s.sub, s.half)
+        for one in between:
+            one.start()
         for k in range(2):
             both = dot(acts[:, k * s.half : (k + 1) * s.half], dgu[...], TN).astype(bf16)
             for n in range(2):
@@ -654,9 +662,10 @@
         greet(in_plane(me) + beside(me) + [twin(me)])
         for one in own:
             one.wait()
+        early(streams, s.late, WARM[:1])
 
     for k in reversed(range(5)):
-        at(k, j - k)
+        at(k, j - k + 1)
 
     @pl.when((j >= 1) & (j <= s.units))
     def _():
@@ -691,9 +700,7 @@
             both = dot(acts[part], weights, NN)
             by = dot(dys[part], ahead, NT).astype(bf16)
             dgu[part, :UNIT], dgu[part, UNIT:], prod[part] = back_gates(both, by)
-        for one in dgu_out(j):
-            one.start()
-        terms.make(j, acts, dgu, prod, dys)
+        terms.make(j, acts, dgu, prod, dys, dgu_out(j))
 
     terms.settle(j)
 
@@ -776,35 +783,30 @@
     return (w - 0.02 * step).astype(bf16), m, v
 
 
+def others(me):
+    steps = [(y, z, c) for y in range(4) for z in range(4) for c in range(2)]
+    return [{"y": ring(me["y"], y), "z": ring(me["z"], z), "c": flip(me["c"] + c)} for y, z, c in steps[1:]]
+
+
 def total_kernel(g0, d0, g1, d1, got, out, sums, sent, here_got):
     me = here()
-    greet(in_plane(me) + [{axis: ring(me[axis], 2)} for axis in ("y", "z")] + [twin(me)])
+    greet(others(me))
     pairs = [remote(g.at[:, 1 - me["c"]], got.at[n], sent.at[n], here_got.at[n], twin(me)) for n, g in enumerate((g0, g1))]
     for one in pairs:
         one.start()
     total = sum(jnp.sum(g[...].astype(f32) ** 2) for g in (g0, d0, g1, d1))
-    total = jnp.full(out.shape, total)
-    base = 0
-    for axis in "cyz":
-        size = lax.axis_size(axis)
-        sums[base] = total
-        copies = []
-        for k in range(1, size):
-            to = {axis: lax.rem(me[axis] + k, size)}
-            copies.append(remote(sums.at[base], sums.at[base + k], sent.at[base + k + 1], here_got.at[base + k + 1], to))
-            copies[-1].start()
-        for k, one in enumerate(copies):
-            one.wait()
-            total += sums[base + k + 1]
-        base += size
-    out[...] = total
+    sums[0] = jnp.full(out.shape, total)
+    for n, to in enumerate(others(me), 1):
+        pairs.append(remote(sums.at[0], sums.at[n], sent.at[n + 1], here_got.at[n + 1], to))
+        pairs[-1].start()
     for one in pairs:
         one.wait()
+    out[...] = jnp.sum(sums[...], 0)
 
 
 def total(number, *sums):
     tile, shape = (8, HALF), sums[0].shape
-    sems = pltpu.SemaphoreType.DMA((12,))
+    sems = pltpu.SemaphoreType.DMA((33,))
     return call(
         total_kernel,
         "total",
@@ -812,7 +814,7 @@
         in_specs=[VMEM] * 4,
         out_specs=[VMEM] * 2,
         out_shape=[array(2, shape[0], *shape[2:]), array(*tile, dtype=f32)],
-        scratch_shapes=[pltpu.VMEM((10, *tile), f32), sems, sems],
+        scratch_shapes=[pltpu.VMEM((32, *tile), f32), sems, sems],
     )(*sums)
 
 
@@ -841,7 +843,8 @@
 
 def finish(s, sums, got, squares, old):
     out = [array(*one.shape, dtype=one.dtype) for one in old]
-    return call(functools.partial(finish_kernel, s), "finish", None, in_specs=[VMEM] * 15, out_specs=[VMEM] * 9, out_shape=out)(*sums, got, squares, *old)
+    kernel = functools.partial(finish_kernel, s)
+    return call(kernel, "finish", None, in_specs=[VMEM] * 15, out_specs=[VMEM] * 9, out_shape=out)(*sums, got, squares, *old)
 
 
 def turned(arrays):
@@ -859,7 +862,7 @@
         gates = gates.reshape(s.layers, s.units, s.pair, PAIR)
         downs = downs.reshape(s.layers, s.units, s.sub, s.d)
         acts0, dys, gu0, prod0, wd0 = first(s, x[0], dy[0], gates, downs)
-        h1, acts1, g_early, d_early = down(s, prod0, wd0.reshape(2, s.ff, s.d), x[0], gates, downs)
+        h1, acts1, g_early, d_early = down(s, prod0, wd0.reshape(s.wide, s.d), x[0], gates, downs)
         dys, acts0, acts1 = (one.reshape(flat) for one in (dys, acts0, acts1))
         dgu1, g_late, theirs, *sums1 = second(s, acts1, dys, gates, downs, g_early, d_early)
         w = (one.reshape(-1, s.d, PAIR) for one in (g_early, g_late, theirs))

time: 685 us -> 644 us (0.940)
  Pallas kernels: 683 us -> 637 us
    pallas_call x3, Pallas kernels: 166 us -> 135 us  [the longest x1 70.1 us: back(): call(functools.partial(back_kernel, s), 'back', 2, grid=(TILES + 1,), in_...]
    pallas_call x1, Pallas kernels: 227 us -> 210 us  [second(): call(functools.partial(second_kernel, s), 'second', 3, grid=(s.units + ST...]
where the time goes in v2:
time: 644 us; the launch traced here: 638 us
  Pallas kernels  637 us (99%)
    pallas_call x1, Pallas kernels, second(): call(functools.partial(second_kernel, s), 'second', 3, grid=(s.units + ST...  210 us
    pallas_call x1, Pallas kernels, third(): call(functools.partial(third_kernel, s), 'third', number, grid=(s.units +...  158 us
    pallas_call x1, Pallas kernels, first(): call(functools.partial(first_kernel, s), 'first', 0, grid=(s.units,), in_...  106 us
    pallas_call x1, Pallas kernels, back(): call(functools.partial(back_kernel, s), 'back', 2, grid=(TILES + 1,), in_...  70.1 us
    pallas_call x1, Pallas kernels, down(): call(functools.partial(down_kernel, s), 'down', 1, grid=(TILES + 1,), in_...  47.1 us
    pallas_call x1, Pallas kernels, finish(): call(kernel, 'finish', None, in_specs=[VMEM] * 15, out_specs=[VMEM] * 9,...  18.1 us
    pallas_call x1, Pallas kernels, total(): call(total_kernel, 'total', number, in_specs=[VMEM] * 4, out_specs=[VMEM]...  15.9 us

profile of v2, /device:TPU:1, one launch (start us, length us, event | category | flops | bytes accessed | tf_op | source)
XLA Modules:
  0.0 637.9 jit_solution(8415984870269925083)
XLA Ops:
  0.6 12.4 %prepare.1 = (bf16[2,9,2,40,512]{4,3,2,1,0:T(8,128)(2,1)}, bf16[2,144,1280]{2,1,0:T(8,128)(2,1)}) custom-call(bf16[2,40,4480]{2,1,0:T(8,128)(2,1)} %refs_0_.1, bf16[2,40,4480]{2,1,0:T(8,128)(2,1)} %refs_1_.1, bf16[140,2,1280]{2,1,0:T(2,128)(2,1)} %bitcast.37), custom_call_target="tpu_custom_call" | custom-call | tf_op jit(solution)/shard_map/prepare/pallas_call | solution.py:276
  13.1 106.2 %first.1 = (bf16[2,2048,1280]{2,1,0:T(8,128)(2,1)}, bf16[2,2048,1280]{2,1,0:T(8,128)(2,1)}, f32[4096,4608]{1,0:T(8,128)}, bf16[2048,4608]{1,0:T(8,128)(2,1)}, bf16[2,9,4,4,16,1280]{5,4,3,2,1,0:T(8,128)(2,1)}) custom-call(bf16[2048,1280]{1,0:T(8,128)(2,1)} %bitcast.23, bf16[2048,1280]{1,0:T(8,128)(2,1)} %bitcast.21, bf16[2,9,80,512]{3,2,1,0:T(8,128)(2,1)} %bitcast.26, ...), custom_call_target="tpu_custom_call" | custom-call | tf_op jit(solution)/shard_map/first/pallas_call | solution.py:384
  119.2 47.1 %down.1 = (bf16[2048,1280]{1,0:T(8,128)(2,1)}, bf16[2,2048,1280]{2,1,0:T(8,128)(2,1)}, bf16[3,4,4,80,512]{4,3,2,1,0:T(8,128)(2,1)}, bf16[3,4,4,16,1280]{4,3,2,1,0:T(8,128)(2,1)}) custom-call(bf16[2048,4608]{1,0:T(8,128)(2,1)} %get-tuple-element.41.prod, bf16[4608,1280]{1,0:T(8,128)(2,1)} %bitcast.18, bf16[2048,1280]{1,0:T(8,128)(2,1)} %bitcast.24, ...), custom_call_target="tpu_custom_call" | custom-call | tf_op jit(solution)/shard_map/down/pallas_call | solution.py:502
  166.3 209.6 %second.1 = (bf16[2048,9216]{1,0:T(8,128)(2,1)}, bf16[6,4,4,80,512]{4,3,2,1,0:T(8,128)(2,1)}, bf16[9,4,4,80,512]{4,3,2,1,0:T(8,128)(2,1)}, bf16[9,2,40,512]{3,2,1,0:T(8,128)(2,1)}, bf16[9,16,1280]{2,1,0:T(8,128)(2,1)}) custom-call(bf16[4096,1280]{1,0:T(8,128)(2,1)} %bitcast.32, bf16[4096,1280]{1,0:T(8,128)(2,1)} %bitcast.31, ...), custom_call_target="tpu_custom_call" | custom-call | tf_op jit(solution)/shard_map/second/pallas_call | solution.py:710
  375.9 70.1 %back.1 = bf16[2,2048,1280]{2,1,0:T(8,128)(2,1)} custom-call(bf16[2048,9216]{1,0:T(8,128)(2,1)} %get-tuple-element.47.dgu, bf16[3,1280,512]{2,1,0:T(8,128)(2,1)} %bitcast.25, bf16[6,1280,512]{2,1,0:T(8,128)(2,1)} %bitcast.33, bf16[9,1280,512]{2,1,0:T(8,128)(2,1)} %bitcast.29, bf16[2048,1280]{1,0:T(8,128)(2,1)} %get-tuple-element.50.h, ...), custom_call_target="tpu_custom_call" | custom-call | tf_op jit(solution)/shard_map/back/pallas_call | solution.py:554
  446.1 157.6 %third.1 = (bf16[9,2,40,512]{3,2,1,0:T(8,128)(2,1)}, bf16[9,16,1280]{2,1,0:T(8,128)(2,1)}) custom-call(bf16[4096,1280]{1,0:T(8,128)(2,1)} %bitcast.30, bf16[4096,1280]{1,0:T(8,128)(2,1)} %bitcast.20, bf16[4608,1280]{1,0:T(8,128)(2,1)} %bitcast.19, f32[4096,4608]{1,0:T(8,128)} %get-tuple-element.51.gu), custom_call_target="tpu_custom_call" | custom-call | tf_op jit(solution)/shard_map/third/pallas_call | solution.py:761
  603.7 15.9 %total.1 = (bf16[2,9,40,512]{3,2,1,0:T(8,128)(2,1)}, f32[8,128]{1,0:T(8,128)}) custom-call(bf16[9,2,40,512]{3,2,1,0:T(8,128)(2,1)} %get-tuple-element.52.g0, bf16[9,16,1280]{2,1,0:T(8,128)(2,1)} %get-tuple-element.53.d0, bf16[9,2,40,512]{3,2,1,0:T(8,128)(2,1)} %get-tuple-element.54.g1, bf16[9,16,1280]{2,1,0:T(8,128)(2,1)} %get-tuple-element.55.d1), custom_call_target="tpu_custom_call" | custom-call | tf_op jit(solution)/shard_map/total/pallas_call | solution.py:810
  619.6 18.1 %finish.1 = (bf16[2,40,4480]{2,1,0:T(8,128)(2,1)}, bf16[2,40,4480]{2,1,0:T(8,128)(2,1)}, bf16[140,2,1280]{2,1,0:T(2,128)(2,1)}, f32[2,40,4480]{2,1,0:T(8,128)}, ...) custom-call(bf16[9,2,40,512]{3,2,1,0:T(8,128)(2,1)} %get-tuple-eleme, ...), custom_call_target="tpu_custom_call" | custom-call | tf_op jit(solution)/shard_map/finish/pallas_call | solution.py:847

commit v3 on v2

--- a/solution.py
+++ b/solution.py
@@ -15,9 +15,10 @@
 UNIT = 256
 PAIR = 2 * UNIT
 PLANE = 4, 4
+CHIPS = 16
 TILES = 8
 ALL = pl.ds(0, 4)
-HALVES = pl.ds(0, 2), pl.ds(2, 2)
+HALVES = [pl.ds(n, 2) for n in (0, 2)]
 EPS = 1e-6
 
 
@@ -30,12 +31,14 @@
     s.layers, s.rows, _ = gate_shape
     s.tokens, s.d = x_shape[1:]
     s.block = down_shape[1]
-    s.padded = -(-s.block // 16) * 16
-    s.ff = 16 * s.padded
+    s.padded = -(-s.block // CHIPS) * CHIPS
+    s.ff = CHIPS * s.padded
     s.units = s.ff // UNIT
-    s.sub = UNIT // 16
+    s.sub = UNIT // CHIPS
     s.early = s.units // 3
     s.late = s.units - s.early
+    s.kept = 3
+    s.summed = s.units - s.kept
     s.pair = 2 * s.rows
     s.both, s.wide, s.tile, s.half = 2 * s.tokens, 2 * s.ff, s.tokens // TILES, s.d // 2
     return s
@@ -53,15 +56,17 @@
     return lax.rem(v, 2)
 
 
-def greet(partners):
+def greet(partners, meanwhile=None):
     barrier = pltpu.get_barrier_semaphore()
     for one in partners:
         pl.semaphore_signal(barrier, inc=1, device_id=one, device_id_type=BY_AXES)
+    if meanwhile:
+        meanwhile()
     pl.semaphore_wait(barrier, len(partners))
 
 
 def in_plane(me):
-    return [{axis: ring(me[axis], k)} for axis in ("y", "z") for k in (1, -1)]
+    return [{axis: ring(me[axis], k)} for axis in "yz" for k in (1, -1)]
 
 
 def beside(me):
@@ -239,7 +244,7 @@
 
 def places(s, core):
     for u in range(s.units):
-        for q in range(16):
+        for q in range(CHIPS):
             n = min(s.sub, s.block - u * s.sub)
             if n > 0:
                 yield u * UNIT + q * s.sub, n, (2 * q + core) * s.block + u * s.sub
@@ -519,18 +524,26 @@
     )(prod, w, h, wg, wd)
 
 
-def back_kernel(s, dgu, w0, w1, w2, h, by, out, wv, local, *refs):
+def back_kernel(s, dgu, w0, w1, w2, h, by, kept_g, kept_d, out, out_g, out_d, wv, local, kept, *refs):
     me = here()
     t = pl.program_id(0)
-    both = Both(s, me, out, *refs)
+    both, terms = Both(s, me, out, *refs[:3]), Terms(s, me, s.kept, out_g, out_d, refs[3:])
     units = [w.at[u] for w in (w0, w1, w2) for u in range(w.shape[0])]
+    loads = [pltpu.make_async_copy(one, wv.at[:, pl.ds(n * PAIR, PAIR)], local.at[n]) for n, one in enumerate(units)]
 
     @pl.when(t == 0)
     def _():
-        loads = [pltpu.make_async_copy(one, wv.at[:, pl.ds(n * PAIR, PAIR)], local.at[n]) for n, one in enumerate(units)]
-        for load in loads:
+        held = [pltpu.make_async_copy(src, term.at[v], sem) for v in range(s.kept) for term, src, sem in terms.kept(v, kept_g, kept_d, kept)]
+        for load in held + loads:
             load.start()
-        greet([twin(me)])
+        greet(in_plane(me) + beside(me) + [twin(me)])
+        for load in held:
+            load.wait()
+
+    terms.settle(t)
+
+    @pl.when(t == 0)
+    def _():
         each = len(units) // 3
         for n in range(3):
             for load in loads[n * each : (n + 1) * each]:
@@ -550,26 +563,32 @@
     both.step(t, lambda: dot(dgu[...], wv[...], NT), make)
 
 
-def back(s, dgu, w0, w1, w2, h, by):
+def back(s, dgu, w0, w1, w2, h, by, *kept):
     return call(
         functools.partial(back_kernel, s),
         "back",
         2,
         grid=(TILES + 1,),
-        in_specs=[tile_spec(s, 2 * s.wide, 0), ANY, ANY, ANY, tile_spec(s, s.d, 1), tile_spec(s, s.d, 1)],
-        out_specs=ANY,
-        out_shape=array(2, s.tokens, s.d),
-        scratch_shapes=[pltpu.VMEM((s.d, 2 * s.wide), bf16), pltpu.SemaphoreType.DMA((2 * s.units,)), *Both.scratch(s)],
-    )(dgu, w0, w1, w2, h, by)
-
-
-def terms_scratch(s):
-    return Scatter.scratch(s.pair, UNIT, s.units) * 2 + Scatter.scratch(s.sub, s.half, s.units) * 2
+        in_specs=[tile_spec(s, 2 * s.wide, 0), ANY, ANY, ANY, tile_spec(s, s.d, 1), tile_spec(s, s.d, 1), ANY, ANY],
+        out_specs=[ANY] + [whole(one.shape) for one in sums(s, s.kept)],
+        out_shape=[array(2, s.tokens, s.d), *sums(s, s.kept)],
+        scratch_shapes=[
+            pltpu.VMEM((s.d, 2 * s.wide), bf16),
+            pltpu.SemaphoreType.DMA((2 * s.units,)),
+            pltpu.SemaphoreType.DMA((s.kept, 4)),
+            *Both.scratch(s),
+            *terms_scratch(s, s.kept),
+        ],
+    )(dgu, w0, w1, w2, h, by, *kept)
+
+
+def terms_scratch(s, units):
+    return Scatter.scratch(s.pair, UNIT, units) * 2 + Scatter.scratch(s.sub, s.half, units) * 2
 
 
 class Terms:
-    def __init__(self, s, me, gates, downs, refs):
-        self.s, self.gates, self.downs = s, gates, downs
+    def __init__(self, s, me, units, gates, downs, refs):
+        self.s, self.units, self.gates, self.downs = s, units, gates, downs
         each = len(refs) // 4
         self.streams = [Scatter(me, refs[n * each : n * each + each - 2], *refs[n * each + each - 2 : n * each + each], *AXES[1 - n % 2]) for n in range(4)]
 
@@ -596,7 +615,7 @@
         for k in reversed(range(STAGES)):
             u = j - k
 
-            @pl.when((u >= 0) & (u < self.s.units))
+            @pl.when((u >= 0) & (u < self.units))
             def _(k=k, u=u):
                 for m in ((0, 1), (2, 3)) if k == 0 else ():
                     for stream in self.streams:
@@ -604,9 +623,12 @@
                 for n, stream in enumerate(self.streams if k else ()):
                     stream.stage(k, u, functools.partial(self.put, n))
 
-
-def sums(s):
-    return [array(s.units, 2, s.rows, PAIR), array(s.units, s.sub, s.d)]
+    def kept(self, v, gates, downs, sems):
+        return [(stream.term, (gates, downs)[n // 2].at[v, n % 2], sems.at[v, n]) for n, stream in enumerate(self.streams)]
+
+
+def sums(s, units):
+    return [array(units, 2, s.rows, PAIR), array(units, s.sub, s.d)]
 
 
 def arrivals(s, sources, targets, sems):
@@ -626,11 +648,12 @@
     return (by * up * (sig + act * (1.0 - sig))).astype(bf16), (by * act).astype(bf16), (act * up).astype(bf16)
 
 
-def second_kernel(s, acts_in, dys_in, wg, wd, g_early, d_early, dgux, g_late, theirs, out_g, out_d, acts, dys, gv, dv, dgu, prod, tiles_in, local, saved, given, sent, *refs):
+def second_kernel(s, acts_in, dys_in, wg, wd, g_early, d_early, dgux, g_late, theirs, kept_g, kept_d, out_g, out_d, acts, dys, gv, dv, dgu, prod, tiles_in, local, saved, given, sent, kept, *refs):
     me = here()
     j = pl.program_id(0)
     streams = streams_of(me, s, gv.at[pl.ds(2, s.late)], dv.at[pl.ds(2, s.late)], refs[:8])
-    terms = Terms(s, me, out_g, out_d, refs[8:])
+    terms = Terms(s, me, s.summed, out_g, out_d, refs[8:])
+    keeps = [[pltpu.make_async_copy(term.at[(s.summed + v) % 3], to, sem) for term, to, sem in terms.kept(v, kept_g, kept_d, kept)] for v in range(s.kept)]
 
     def at(k, u):
         at_stage(streams, k, u, s.late)
@@ -702,7 +725,23 @@
             dgu[part, :UNIT], dgu[part, UNIT:], prod[part] = back_gates(both, by)
         terms.make(j, acts, dgu, prod, dys, dgu_out(j))
 
+    for v, copies in enumerate(keeps):
+
+        @pl.when(j == s.summed + v)
+        def _(copies=copies):
+            for one in copies:
+                one.start()
+
     terms.settle(j)
+
+    @pl.when(j == s.units)
+    def _():
+        for one in sum(keeps, []):
+            one.wait()
+
+
+def kept_shapes(s):
+    return [array(s.kept, 2, *PLANE, s.pair, UNIT), array(s.kept, 2, *PLANE, s.sub, s.half)]
 
 
 def second(s, acts, dys, wg, wd, g_early, d_early):
@@ -711,10 +750,10 @@
         functools.partial(second_kernel, s),
         "second",
         3,
-        grid=(s.units + STAGES - 1,),
+        grid=(s.summed + STAGES - 1,),
         in_specs=[ANY] * 6,
-        out_specs=[ANY] * 3 + [whole(one.shape) for one in sums(s)],
-        out_shape=[array(s.tokens, 2 * s.wide), array(s.late, *unit), array(s.units, *unit), *sums(s)],
+        out_specs=[ANY] * 5 + [whole(one.shape) for one in sums(s, s.summed)],
+        out_shape=[array(s.tokens, 2 * s.wide), array(s.late, *unit), array(s.units, *unit), *kept_shapes(s), *sums(s, s.summed)],
         scratch_shapes=[
             *[pltpu.VMEM((s.both, s.d), bf16)] * 2,
             pltpu.VMEM((2 + s.late, *unit), bf16),
@@ -726,8 +765,9 @@
             pltpu.SemaphoreType.DMA,
             pltpu.SemaphoreType.DMA((2, s.units)),
             pltpu.SemaphoreType.DMA((3, s.units)),
+            pltpu.SemaphoreType.DMA((s.kept, 4)),
             *gather_sems(s.late),
-            *terms_scratch(s),
+            *terms_scratch(s, s.summed),
         ],
     )(acts, dys, wg, wd, g_early, d_early)
 
@@ -735,7 +775,7 @@
 def third_kernel(s, acts_in, dh_in, wd, gu, out_g, out_d, acts, dh, dgu, prod, tiles_in, *refs):
     me = here()
     j = pl.program_id(0)
-    terms = Terms(s, me, out_g, out_d, refs)
+    terms = Terms(s, me, s.units, out_g, out_d, refs)
     arrive = arrivals(s, (dh_in, acts_in), (dh, acts), tiles_in)
 
     @pl.when(j == 0)
@@ -764,14 +804,14 @@
         number,
         grid=(s.units + STAGES - 1,),
         in_specs=[ANY] * 2 + [pl.BlockSpec((UNIT, s.d), lambda j: (at(j), 0)), pl.BlockSpec((s.both, PAIR), lambda j: (0, at(j)))],
-        out_specs=[whole(one.shape) for one in sums(s)],
-        out_shape=sums(s),
+        out_specs=[whole(one.shape) for one in sums(s, s.units)],
+        out_shape=sums(s, s.units),
         scratch_shapes=[
             *[pltpu.VMEM((s.both, s.d), bf16)] * 2,
             pltpu.VMEM((s.both, PAIR), bf16),
             pltpu.VMEM((s.both, UNIT), bf16),
             pltpu.SemaphoreType.DMA((4, 2)),
-            *terms_scratch(s),
+            *terms_scratch(s, s.units),
         ],
     )(acts, dh, wd, gu)
 
@@ -788,63 +828,85 @@
     return [{"y": ring(me["y"], y), "z": ring(me["z"], z), "c": flip(me["c"] + c)} for y, z, c in steps[1:]]
 
 
-def total_kernel(g0, d0, g1, d1, got, out, sums, sent, here_got):
+def total_kernel(s, g0, d0, g1, d1, g2, d2, out, squares, sums, got0, got1, got2, sent, here_got):
     me = here()
-    greet(others(me))
-    pairs = [remote(g.at[:, 1 - me["c"]], got.at[n], sent.at[n], here_got.at[n], twin(me)) for n, g in enumerate((g0, g1))]
+    c = me["c"]
+
+    def add_up():
+        total = sum(jnp.sum(g[...].astype(f32) ** 2) for g in (g0, d0, g1, d1, g2, d2))
+        sums[0] = jnp.full(squares.shape, total)
+
+    greet(others(me), add_up)
+    exchanged = (g0, got0), (g1, got1), (g2, got2)
+    pairs = [remote(g.at[:, 1 - c], got, sent.at[n], here_got.at[n], twin(me)) for n, (g, got) in enumerate(exchanged)]
     for one in pairs:
         one.start()
-    total = sum(jnp.sum(g[...].astype(f32) ** 2) for g in (g0, d0, g1, d1))
-    sums[0] = jnp.full(out.shape, total)
-    for n, to in enumerate(others(me), 1):
-        pairs.append(remote(sums.at[0], sums.at[n], sent.at[n + 1], here_got.at[n + 1], to))
-        pairs[-1].start()
+    copies = [remote(sums.at[0], sums.at[n], sent.at[n + 2], here_got.at[n + 2], to) for n, to in enumerate(others(me), 1)]
+    for one in copies:
+        one.start()
     for one in pairs:
         one.wait()
-    out[...] = jnp.sum(sums[...], 0)
-
-
-def total(number, *sums):
-    tile, shape = (8, HALF), sums[0].shape
-    sems = pltpu.SemaphoreType.DMA((33,))
+    moves = [(start, n, core * s.ff + to) for core in range(2) for to, n, start in places(s, core)]
+    for layer, refs in enumerate((exchanged[:1], exchanged[1:])):
+        for mat in range(2):
+            lanes = pl.ds(mat * UNIT, UNIT)
+            mine = jnp.concatenate([g[u, c, :, lanes] for g, _ in refs for u in range(g.shape[0])], 1).astype(f32)
+            other = jnp.concatenate([got[u, :, lanes] for _, got in refs for u in range(got.shape[0])], 1).astype(f32)
+            both = jnp.concatenate([jnp.where(c == 0, mine, other), jnp.where(c == 0, other, mine)], 1)
+            out[layer, mat] = jnp.concatenate(tiles(both, 32 * s.block, moves), 1).astype(bf16)
+    for one in copies:
+        one.wait()
+    squares[...] = jnp.sum(sums[...], 0)
+
+
+def total(s, number, *sums):
+    tile = (8, HALF)
+    sems = pltpu.SemaphoreType.DMA((34,))
     return call(
-        total_kernel,
+        functools.partial(total_kernel, s),
         "total",
         number,
-        in_specs=[VMEM] * 4,
+        in_specs=[VMEM] * 6,
         out_specs=[VMEM] * 2,
-        out_shape=[array(2, shape[0], *shape[2:]), array(*tile, dtype=f32)],
-        scratch_shapes=[pltpu.VMEM((32, *tile), f32), sems, sems],
+        out_shape=[array(s.layers, 2, s.rows, 32 * s.block), array(*tile, dtype=f32)],
+        scratch_shapes=[pltpu.VMEM((32, *tile), f32), *[pltpu.VMEM((g.shape[0], *g.shape[2:]), bf16) for g in sums[::2]], sems, sems],
     )(*sums)
 
 
-def finish_kernel(s, g0, d0, g1, d1, got, squares, *refs):
-    old, new = refs[:9], refs[9:]
-    c = lax.axis_index("c")
-    count = 16 * (s.layers * s.pair * 32 * s.block * 3)
+def finish_kernel(s, g, d0, d1, d2, squares, *refs):
+    old, new, bufs, (ins, outs) = refs[:9], refs[9:18], refs[18:27], refs[27:]
+    loads = [pltpu.make_async_copy(src, dst, ins.at[n]) for n, (src, dst) in enumerate(zip(old, bufs, strict=True))]
+    stores = [pltpu.make_async_copy(src, dst, outs.at[n]) for n, (src, dst) in enumerate(zip(bufs, new, strict=True))]
+    for n in range(3):
+        for load in loads[n::3]:
+            load.start()
+    count = s.layers * s.d * 32 * s.block * 3
     factor = jnp.minimum(1.0, 0.5 * lax.rsqrt(squares[:1, :1] / count + 1e-30))
-    moves = [(start, n, core * s.ff + to) for core in range(2) for to, n, start in places(s, core)]
-
-    def update(n, at, g):
-        w, m, v = (old[n + 3 * k] for k in range(3))
-        made = adamw(w[at].astype(f32), m[at], v[at], g * factor)
-        for k, value in enumerate(made):
-            new[n + 3 * k][at] = value
-
-    for layer, (g, d) in enumerate(((g0, d0), (g1, d1))):
-        for mat in range(2):
-            lanes = pl.ds(mat * UNIT, UNIT)
-            pieces = [[ref[u, c, :, lanes] if ref is g else ref[layer, u, :, lanes] for u in range(s.units)] for ref in (g, got)]
-            mine, other = (jnp.concatenate(piece, 1).astype(f32) for piece in pieces)
-            both = jnp.concatenate([jnp.where(c == 0, mine, other), jnp.where(c == 0, other, mine)], 1)
-            update(mat, layer, jnp.concatenate(tiles(both, 32 * s.block, moves), 1))
-        update(2, (slice(None), layer), d[...].astype(f32).reshape(s.padded, s.d)[: s.block])
-
-
-def finish(s, sums, got, squares, old):
+    for n in range(3):
+        for load in loads[n::3]:
+            load.wait()
+        for layer in range(s.layers):
+            if n < 2:
+                at, grad = layer, g[layer, n].astype(f32)
+            else:
+                rows = jnp.concatenate([one[...] for one in ((d1, d2) if layer else (d0,))], 0).reshape(s.padded, s.d)
+                at, grad = (slice(None), layer), rows[: s.block].astype(f32)
+            w, m, v = bufs[n::3]
+            made = adamw(w[at].astype(f32), m[at], v[at], grad * factor)
+            for ref, value in zip((w, m, v), made, strict=True):
+                ref[at] = value
+        for store in stores[n::3]:
+            store.start()
+    for store in stores:
+        store.wait()
+
+
+def finish(s, g, downs, squares, old):
     out = [array(*one.shape, dtype=one.dtype) for one in old]
+    sems = pltpu.SemaphoreType.DMA((9,))
     kernel = functools.partial(finish_kernel, s)
-    return call(kernel, "finish", None, in_specs=[VMEM] * 15, out_specs=[VMEM] * 9, out_shape=out)(*sums, got, squares, *old)
+    scratch = [pltpu.VMEM(one.shape, one.dtype) for one in old] + [sems, sems]
+    return call(kernel, "finish", None, in_specs=[VMEM] * 5 + [ANY] * 9, out_specs=[ANY] * 9, out_shape=out, scratch_shapes=scratch)(g, *downs, squares, *old)
 
 
 def turned(arrays):
@@ -864,11 +926,14 @@
         acts0, dys, gu0, prod0, wd0 = first(s, x[0], dy[0], gates, downs)
         h1, acts1, g_early, d_early = down(s, prod0, wd0.reshape(s.wide, s.d), x[0], gates, downs)
         dys, acts0, acts1 = (one.reshape(flat) for one in (dys, acts0, acts1))
-        dgu1, g_late, theirs, *sums1 = second(s, acts1, dys, gates, downs, g_early, d_early)
+        dgu1, g_late, theirs, kept_g, kept_d, *sums1 = second(s, acts1, dys, gates, downs, g_early, d_early)
         w = (one.reshape(-1, s.d, PAIR) for one in (g_early, g_late, theirs))
-        dh = back(s, dgu1, *w, h1, dy[0]).reshape(flat)
+        dh, *sums2 = back(s, dgu1, *w, h1, dy[0], kept_g, kept_d)
+        dh = dh.reshape(flat)
         sums0 = third(s, 6, acts0, dh, wd0.reshape(-1, s.d), gu0)
-        return tuple(turned(finish(s, (*sums0, *sums1), *total(7, *sums0, *sums1), arrays)))
+        every = (*sums0, *sums1, *sums2)
+        g, squares = total(s, 7, *every)
+        return tuple(turned(finish(s, g, every[1::2], squares, arrays)))
 
     place = ("y", "z", "c")
     states, cut = P(("rep", "x", *place), None, None), P(None, place, None)

time: 644 us -> 633 us (0.983)
  Pallas kernels: 637 us -> 626 us
    pallas_call x3, Pallas kernels: 244 us -> 221 us  [the longest x1 190 us: second(): call(functools.partial(second_kernel, s), 'second', 3, grid=(s.summed + S...]
    pallas_call x1, Pallas kernels: 70.1 us -> 82.2 us  [back(): call(functools.partial(back_kernel, s), 'back', 2, grid=(TILES + 1,), in_...]
where the time goes in v3:
time: 633 us; the launch traced here: 627 us
  Pallas kernels  626 us (99%)
    pallas_call x1, Pallas kernels, second(): call(functools.partial(second_kernel, s), 'second', 3, grid=(s.summed + S...  190 us
    pallas_call x1, Pallas kernels, third(): call(functools.partial(third_kernel, s), 'third', number, grid=(s.units +...  157 us
    pallas_call x1, Pallas kernels, first(): call(functools.partial(first_kernel, s), 'first', 0, grid=(s.units,), in_...  106 us
    pallas_call x1, Pallas kernels, back(): call(functools.partial(back_kernel, s), 'back', 2, grid=(TILES + 1,), in_...  82.2 us
    pallas_call x1, Pallas kernels, down(): call(functools.partial(down_kernel, s), 'down', 1, grid=(TILES + 1,), in_...  47.1 us
    pallas_call x1, Pallas kernels, total(): call(functools.partial(total_kernel, s), 'total', number, in_specs=[VMEM]...  18.2 us

profile of v3, /device:TPU:1, one launch (start us, length us, event | category | flops | bytes accessed | tf_op | source)
XLA Modules:
  0.0 627.0 jit_solution(15140762175267719728)
XLA Ops:
  0.6 12.4 %prepare.1 = (bf16[2,9,2,40,512]{4,3,2,1,0:T(8,128)(2,1)}, bf16[2,144,1280]{2,1,0:T(8,128)(2,1)}) custom-call(bf16[2,40,4480]{2,1,0:T(8,128)(2,1)} %refs_0_.1, bf16[2,40,4480]{2,1,0:T(8,128)(2,1)} %refs_1_.1, bf16[140,2,1280]{2,1,0:T(2,128)(2,1)} %bitcast.37), custom_call_target="tpu_custom_call" | custom-call | tf_op jit(solution)/shard_map/prepare/pallas_call | solution.py:281
  13.1 106.2 %first.1 = (bf16[2,2048,1280]{2,1,0:T(8,128)(2,1)}, bf16[2,2048,1280]{2,1,0:T(8,128)(2,1)}, f32[4096,4608]{1,0:T(8,128)}, bf16[2048,4608]{1,0:T(8,128)(2,1)}, bf16[2,9,4,4,16,1280]{5,4,3,2,1,0:T(8,128)(2,1)}) custom-call(bf16[2048,1280]{1,0:T(8,128)(2,1)} %bitcast.22, bf16[2048,1280]{1,0:T(8,128)(2,1)} %bitcast.20, bf16[2,9,80,512]{3,2,1,0:T(8,128)(2,1)} %bitcast.25, ...), custom_call_target="tpu_custom_call" | custom-call | tf_op jit(solution)/shard_map/first/pallas_call | solution.py:389
  119.2 47.1 %down.1 = (bf16[2048,1280]{1,0:T(8,128)(2,1)}, bf16[2,2048,1280]{2,1,0:T(8,128)(2,1)}, bf16[3,4,4,80,512]{4,3,2,1,0:T(8,128)(2,1)}, bf16[3,4,4,16,1280]{4,3,2,1,0:T(8,128)(2,1)}) custom-call(bf16[2048,4608]{1,0:T(8,128)(2,1)} %get-tuple-element.46.prod, bf16[4608,1280]{1,0:T(8,128)(2,1)} %bitcast.18, bf16[2048,1280]{1,0:T(8,128)(2,1)} %bitcast.23, ...), custom_call_target="tpu_custom_call" | custom-call | tf_op jit(solution)/shard_map/down/pallas_call | solution.py:507
  166.3 190.3 %second.1 = (bf16[2048,9216]{1,0:T(8,128)(2,1)}, bf16[6,4,4,80,512]{4,3,2,1,0:T(8,128)(2,1)}, bf16[9,4,4,80,512]{4,3,2,1,0:T(8,128)(2,1)}, bf16[3,2,4,4,80,256]{...) custom-call(bf16[4096,1280]{1,0:T(8,128)(2,1)} %bitcast.32, ...), custom_call_target="tpu_custom_call" | custom-call | tf_op jit(solution)/shard_map/second/pallas_call | solution.py:749
  356.7 82.2 %back.1 = (bf16[2,2048,1280]{2,1,0:T(8,128)(2,1)}, bf16[3,2,40,512]{3,2,1,0:T(8,128)(2,1)}, bf16[3,16,1280]{2,1,0:T(8,128)(2,1)}) custom-call(bf16[2048,9216]{1,0:T(8,128)(2,1)} %get-tuple-element.52.dgu, bf16[3,1280,512]{2,1,0:T(8,128)(2,1)} %bitcast.24, bf16[6,1280,512]{2,1,0:T(8,128)(2,1)} %bitcast.33, bf16[9,1280,512]{2,1,0:T(8,128)(2,1)} %bitcast.28, ...), custom_call_target="tpu_custom_call" | custom-call | tf_op jit(solution)/shard_map/back/pallas_call | solution.py:567
  438.9 157.2 %third.1 = (bf16[9,2,40,512]{3,2,1,0:T(8,128)(2,1)}, bf16[9,16,1280]{2,1,0:T(8,128)(2,1)}) custom-call(bf16[4096,1280]{1,0:T(8,128)(2,1)} %bitcast.29, bf16[4096,1280]{1,0:T(8,128)(2,1)} %bitcast.30, bf16[4608,1280]{1,0:T(8,128)(2,1)} %bitcast.19, f32[4096,4608]{1,0:T(8,128)} %get-tuple-element.59.gu), custom_call_target="tpu_custom_call" | custom-call | tf_op jit(solution)/shard_map/third/pallas_call | solution.py:801
  596.1 18.2 %total.1 = (bf16[2,2,40,4480]{3,2,1,0:T(8,128)(2,1)}, f32[8,128]{1,0:T(8,128)}) custom-call(bf16[9,2,40,512]{3,2,1,0:T(8,128)(2,1)} %get-tuple-element.60.g0, bf16[9,16,1280]{2,1,0:T(8,128)(2,1)} %get-tuple-element.61.d0, bf16[6,2,40,512]{3,2,1,0:T(8,128)(2,1)} %get-tuple-element.62.g1, bf16[6,16,1280]{2,1,0:T(8,128)(2,1)} %get-tuple-element.63.d1, ...), custom_call_target="tpu_custom_call" | custom-call | tf_op jit(solution)/shard_map/total/pallas_call | solution.py:865
  614.3 12.5 %finish.1 = (bf16[2,40,4480]{2,1,0:T(8,128)(2,1)}, bf16[2,40,4480]{2,1,0:T(8,128)(2,1)}, bf16[140,2,1280]{2,1,0:T(2,128)(2,1)}, f32[2,40,4480]{2,1,0:T(8,128)}, ...) custom-call(bf16[2,2,40,4480]{3,2,1,0:T(8,128)(2,1)} %get-tuple-elem, ...), custom_call_target="tpu_custom_call" | custom-call | tf_op jit(solution)/shard_map/finish/pallas_call | solution.py:909

commit v4 on v3

--- a/solution.py
+++ b/solution.py
@@ -252,13 +252,16 @@
 
 def prepare_kernel(s, wg, wu, wd, gates, downs, halves, padded, sems):
     me = here()
-    greet([twin(me)])
-    for layer in range(s.layers):
-        for mat, w in enumerate((wg, wu)):
-            for core in range(2):
-                for k, tile in enumerate(tiles(w[layer].astype(f32), s.ff, places(s, core))):
-                    halves[core, layer, k // 2, :, pl.ds(mat * UNIT + k % 2 * HALF, HALF)] = tile.astype(bf16)
-        padded[layer] = jnp.concatenate([wd[:, layer], jnp.zeros((s.padded - s.block, s.d), bf16)], 0)
+
+    def arrange():
+        for layer in range(s.layers):
+            for mat, w in enumerate((wg, wu)):
+                for core in range(2):
+                    for k, tile in enumerate(tiles(w[layer].astype(f32), s.ff, places(s, core))):
+                        halves[core, layer, k // 2, :, pl.ds(mat * UNIT + k % 2 * HALF, HALF)] = tile.astype(bf16)
+            padded[layer] = jnp.concatenate([wd[:, layer], jnp.zeros((s.padded - s.block, s.d), bf16)], 0)
+
+    greet([twin(me)], arrange)
     c = me["c"]
     give = remote(halves.at[1 - c], gates.at[:, :, c], sems.at[0], sems.at[1], twin(me))
     keep = pltpu.make_async_copy(halves.at[c], gates.at[:, :, c], sems.at[2])
@@ -531,12 +534,21 @@
     units = [w.at[u] for w in (w0, w1, w2) for u in range(w.shape[0])]
     loads = [pltpu.make_async_copy(one, wv.at[:, pl.ds(n * PAIR, PAIR)], local.at[n]) for n, one in enumerate(units)]
 
+    each = len(units) // 3
+
+    def third_of_first(n):
+        for load in loads[n * each : (n + 1) * each]:
+            load.wait()
+        part = pl.ds(n * each * PAIR, each * PAIR)
+        product = dot(dgu[:, part], wv[:, part], NT)
+        both.total[...] = both.total[...] + product if n else product
+
     @pl.when(t == 0)
     def _():
         held = [pltpu.make_async_copy(src, term.at[v], sem) for v in range(s.kept) for term, src, sem in terms.kept(v, kept_g, kept_d, kept)]
-        for load in held + loads:
+        for load in loads[:each] + held + loads[each:]:
             load.start()
-        greet(in_plane(me) + beside(me) + [twin(me)])
+        greet(in_plane(me) + beside(me) + [twin(me)], lambda: third_of_first(0))
         for load in held:
             load.wait()
 
@@ -544,13 +556,8 @@
 
     @pl.when(t == 0)
     def _():
-        each = len(units) // 3
-        for n in range(3):
-            for load in loads[n * each : (n + 1) * each]:
-                load.wait()
-            part = pl.ds(n * each * PAIR, each * PAIR)
-            product = dot(dgu[:, part], wv[:, part], NT)
-            both.total[...] = both.total[...] + product if n else product
+        third_of_first(1)
+        third_of_first(2)
 
     def make(total):
         da = total.astype(bf16).astype(f32)

time: 633 us -> 630 us (level)
  no operation moved by 1% of the time
where the time goes in v4:
time: 630 us; the launch traced here: 624 us
  Pallas kernels  623 us (99%)
    pallas_call x1, Pallas kernels, second(): call(functools.partial(second_kernel, s), 'second', 3, grid=(s.summed + S...  190 us
    pallas_call x1, Pallas kernels, third(): call(functools.partial(third_kernel, s), 'third', number, grid=(s.units +...  156 us
    pallas_call x1, Pallas kernels, first(): call(functools.partial(first_kernel, s), 'first', 0, grid=(s.units,), in_...  106 us
    pallas_call x1, Pallas kernels, back(): call(functools.partial(back_kernel, s), 'back', 2, grid=(TILES + 1,), in_...  81.4 us
    pallas_call x1, Pallas kernels, down(): call(functools.partial(down_kernel, s), 'down', 1, grid=(TILES + 1,), in_...  47.1 us
    pallas_call x1, Pallas kernels, total(): call(functools.partial(total_kernel, s), 'total', number, in_specs=[VMEM]...  18.2 us

profile of v4, /device:TPU:1, one launch (start us, length us, event | category | flops | bytes accessed | tf_op | source)
XLA Modules:
  0.0 624.4 jit_solution(11023561855877809494)
XLA Ops:
  0.6 12.2 %prepare.1 = (bf16[2,9,2,40,512]{4,3,2,1,0:T(8,128)(2,1)}, bf16[2,144,1280]{2,1,0:T(8,128)(2,1)}) custom-call(bf16[2,40,4480]{2,1,0:T(8,128)(2,1)} %refs_0_.1, bf16[2,40,4480]{2,1,0:T(8,128)(2,1)} %refs_1_.1, bf16[140,2,1280]{2,1,0:T(2,128)(2,1)} %bitcast.37), custom_call_target="tpu_custom_call" | custom-call | tf_op jit(solution)/shard_map/prepare/pallas_call | solution.py:284
  12.9 105.8 %first.1 = (bf16[2,2048,1280]{2,1,0:T(8,128)(2,1)}, bf16[2,2048,1280]{2,1,0:T(8,128)(2,1)}, f32[4096,4608]{1,0:T(8,128)}, bf16[2048,4608]{1,0:T(8,128)(2,1)}, bf16[2,9,4,4,16,1280]{5,4,3,2,1,0:T(8,128)(2,1)}) custom-call(bf16[2048,1280]{1,0:T(8,128)(2,1)} %bitcast.22, bf16[2048,1280]{1,0:T(8,128)(2,1)} %bitcast.20, bf16[2,9,80,512]{3,2,1,0:T(8,128)(2,1)} %bitcast.25, ...), custom_call_target="tpu_custom_call" | custom-call | tf_op jit(solution)/shard_map/first/pallas_call | solution.py:392
  118.7 47.1 %down.1 = (bf16[2048,1280]{1,0:T(8,128)(2,1)}, bf16[2,2048,1280]{2,1,0:T(8,128)(2,1)}, bf16[3,4,4,80,512]{4,3,2,1,0:T(8,128)(2,1)}, bf16[3,4,4,16,1280]{4,3,2,1,0:T(8,128)(2,1)}) custom-call(bf16[2048,4608]{1,0:T(8,128)(2,1)} %get-tuple-element.46.prod, bf16[4608,1280]{1,0:T(8,128)(2,1)} %bitcast.18, bf16[2048,1280]{1,0:T(8,128)(2,1)} %bitcast.23, ...), custom_call_target="tpu_custom_call" | custom-call | tf_op jit(solution)/shard_map/down/pallas_call | solution.py:510
  165.8 190.4 %second.1 = (bf16[2048,9216]{1,0:T(8,128)(2,1)}, bf16[6,4,4,80,512]{4,3,2,1,0:T(8,128)(2,1)}, bf16[9,4,4,80,512]{4,3,2,1,0:T(8,128)(2,1)}, bf16[3,2,4,4,80,256]{...) custom-call(bf16[4096,1280]{1,0:T(8,128)(2,1)} %bitcast.32, ...), custom_call_target="tpu_custom_call" | custom-call | tf_op jit(solution)/shard_map/second/pallas_call | solution.py:756
  356.2 81.4 %back.1 = (bf16[2,2048,1280]{2,1,0:T(8,128)(2,1)}, bf16[3,2,40,512]{3,2,1,0:T(8,128)(2,1)}, bf16[3,16,1280]{2,1,0:T(8,128)(2,1)}) custom-call(bf16[2048,9216]{1,0:T(8,128)(2,1)} %get-tuple-element.52.dgu, bf16[3,1280,512]{2,1,0:T(8,128)(2,1)} %bitcast.24, bf16[6,1280,512]{2,1,0:T(8,128)(2,1)} %bitcast.33, bf16[9,1280,512]{2,1,0:T(8,128)(2,1)} %bitcast.28, ...), custom_call_target="tpu_custom_call" | custom-call | tf_op jit(solution)/shard_map/back/pallas_call | solution.py:574
  437.6 155.9 %third.1 = (bf16[9,2,40,512]{3,2,1,0:T(8,128)(2,1)}, bf16[9,16,1280]{2,1,0:T(8,128)(2,1)}) custom-call(bf16[4096,1280]{1,0:T(8,128)(2,1)} %bitcast.29, bf16[4096,1280]{1,0:T(8,128)(2,1)} %bitcast.30, bf16[4608,1280]{1,0:T(8,128)(2,1)} %bitcast.19, f32[4096,4608]{1,0:T(8,128)} %get-tuple-element.59.gu), custom_call_target="tpu_custom_call" | custom-call | tf_op jit(solution)/shard_map/third/pallas_call | solution.py:808
  593.5 18.2 %total.1 = (bf16[2,2,40,4480]{3,2,1,0:T(8,128)(2,1)}, f32[8,128]{1,0:T(8,128)}) custom-call(bf16[9,2,40,512]{3,2,1,0:T(8,128)(2,1)} %get-tuple-element.60.g0, bf16[9,16,1280]{2,1,0:T(8,128)(2,1)} %get-tuple-element.61.d0, bf16[6,2,40,512]{3,2,1,0:T(8,128)(2,1)} %get-tuple-element.62.g1, bf16[6,16,1280]{2,1,0:T(8,128)(2,1)} %get-tuple-element.63.d1, ...), custom_call_target="tpu_custom_call" | custom-call | tf_op jit(solution)/shard_map/total/pallas_call | solution.py:872
  611.7 12.5 %finish.1 = (bf16[2,40,4480]{2,1,0:T(8,128)(2,1)}, bf16[2,40,4480]{2,1,0:T(8,128)(2,1)}, bf16[140,2,1280]{2,1,0:T(2,128)(2,1)}, f32[2,40,4480]{2,1,0:T(8,128)}, ...) custom-call(bf16[2,2,40,4480]{3,2,1,0:T(8,128)(2,1)} %get-tuple-elem, ...), custom_call_target="tpu_custom_call" | custom-call | tf_op jit(solution)/shard_map/finish/pallas_call | solution.py:916
